TPU v7x, 16 devices: a 4x2x1 block of a 4x4x8 slice. The times are simulated.
16 devices in a mesh: kv: 2 (over y, z), dup: 8 (over x, core).
Axes of the slice: x: 4, y: 2, z: 1, core: 2. Of those that a mesh axis runs over, the one named last changes fastest.
The devices are a block of a 4x4x8 slice.
Arguments:
- queries: bfloat16 [512, 24, 128], P('kv', 'dup'), parts along dimension 0
- key_cache: bfloat16 [512, 4096, 128], P('kv', 'dup'), parts along dimension 0
- value_cache: bfloat16 [512, 4096, 128], P('kv', 'dup'), parts along dimension 0
- lengths: int32 [512], P('kv'), parts along dimension 0
Outputs:
- output: bfloat16 [512, 24, 128], P('kv', 'dup'), parts along dimension 0
There are 2 independent parts. A program takes and returns all parts, laid end to end along the dimension named above; each array names one.
All inputs are finite; a program needn't handle non-finite values.
Results may differ from a plain program's by a relative error of at most 0.00823596.
Values are sent between devices in bfloat16 or wider.
A program may use at most 768 MiB of HBM per device.

v0:
```python
import jax
import jax.numpy as jnp
from jax import lax
from jax.sharding import PartitionSpec as P, NamedSharding

DRAFT = 4
NEG_BIG = -1e30


def solution(mesh):
    dup_size = mesh.shape["dup"]

    def group_step(q_local, k_span, v_span, len_local):
        num_batch, span_len, head_dim = k_span.shape
        span_start = lax.axis_index("dup") * span_len
        q_group = lax.all_gather(q_local, "dup", axis=1, tiled=True)
        num_rows = q_group.shape[1]
        own_rows = num_rows // dup_size
        scores = jnp.einsum("brd,bsd->brs", q_group, k_span, preferred_element_type=jnp.float32) * (head_dim ** -0.5)
        last_pos = len_local[:, None] - DRAFT + (jnp.arange(num_rows) % DRAFT)[None, :]
        allowed = (span_start + jnp.arange(span_len))[None, None, :] <= last_pos[:, :, None]
        scores = jnp.where(allowed, scores, NEG_BIG)
        row_peak = jnp.max(scores, axis=2, keepdims=True)
        prob_vals = jnp.exp(scores - row_peak)
        row_mass = jnp.sum(prob_vals, axis=2, keepdims=True)
        weighted = jnp.einsum("brs,bsd->brd", prob_vals.astype(jnp.bfloat16), v_span, preferred_element_type=jnp.float32)
        part_out = (weighted / row_mass).astype(jnp.bfloat16).reshape(num_batch, dup_size, own_rows, head_dim)
        log_mass = (row_peak + jnp.log(row_mass)).reshape(num_batch, dup_size, own_rows)
        recv_out = lax.all_to_all(part_out, "dup", 1, 1)
        recv_mass = lax.all_to_all(log_mass, "dup", 1, 1)
        top_mass = jnp.max(recv_mass, axis=1, keepdims=True)
        weights = jnp.exp(recv_mass - top_mass)
        total_mass = jnp.sum(weights, axis=1)
        merged = jnp.sum(weights[..., None] * recv_out.astype(jnp.float32), axis=1)
        return (merged / total_mass[..., None]).astype(jnp.bfloat16)

    return jax.shard_map(group_step, mesh=mesh, in_specs=(P("kv", "dup", None), P("kv", "dup", None), P("kv", "dup", None), P("kv")), out_specs=P("kv", "dup", None), check_vma=False)
```

profile of v0, /device:TPU:112, one launch (start us, length us, event | category | flops | bytes accessed | tf_op | source)
XLA Modules:
  0.0 122.2 jit_solution(7731956329083310167)
XLA Ops:
  6.5 0.0 all-gather.2.cloned.1.call-start
  6.6 0.7 all-gather.2.cloned.1.call-update
  7.3 0.7 broadcast_add_fusion.1
  8.0 0.1 broadcast_add_fusion
  8.1 23.9 %all-gather.2.cloned.1.call-done = bf16[256,24,128]{2,0,1:T(8,128)(2,1)} async-done(((bf16[256,3,128]{2,0,1:T(8,128)(2,1)}), bf16[256,24,128]{2,0,1:T(8,128)(2,1)}) %all-gather.2.cloned.1.call-update) | async-done | bytes 1572880 | tf_op jit(solution)/shard_map/all_gather | solution.py:16
  32.0 24.8 %fusion.2 = (f32[256,24]{1,0:T(8,128)S(1)}, f32[256,24,512]{2,1,0:T(8,128)}) fusion(s32[256,24]{1,0:T(8,128)S(1)} %broadcast_add_fusion, s32[512]{0:T(512)S(1)} %iota_add_fusion, bf16[256,512,128]{2,1,0:T(8,128)(2,1)} %param.5, bf16[256,24,128]{2,0,1:T(8,128)(2,1)} %all-gather.2.cloned.1.call-done), kind=kOutput, calls=%fused_computation.4 | convolution fusion | flops 817883136 | bytes 47761408 | tf_op jit(solution)/shard_map/brd,bsd->brs/dot_general | solution.py:19
  56.8 0.1 copy.15
  56.9 7.2 %fusion.1 = f32[256,24]{1,0:T(8,128)S(1)} fusion(f32[256,24,512]{2,1,0:T(8,128)} %get-tuple-element.8, f32[256,24]{1,0:T(8,128)S(1)} %get-tuple-element.7, s32[256,24]{1,0:T(8,128)S(1)} %broadcast_add_fusion, s32[512]{0:T(512)S(1)} %iota_add_fusion), kind=kLoop, calls=%fused_computation.3 | loop fusion | flops 15722496 | bytes 12658688 | tf_op jit(solution)/shard_map/reduce_sum | solution.py:25
  64.2 0.1 copy.14
  64.2 0.6 add.55
  64.9 3.5 %all-to-all-start = ((f32[256,8,3]{0,2,1:T(4,128)}), f32[256,8,3]{0,2,1:T(4,128)S(1)}, u32[]{:S(2)}, u32[]{:S(2)}) async-start(f32[256,8,3]{0,2,1:T(4,128)} %add.55), calls=%async_computation | async-start | bytes 65536 | tf_op jit(solution)/shard_map/all_to_all | solution.py:30
  68.4 17.4 %divide_convert_fusion = bf16[256,24,128]{2,1,0:T(8,128)(2,1)S(1)} fusion(f32[256,24]{1,0:T(8,128)S(1)} %fusion.1, bf16[256,512,128]{2,1,0:T(8,128)(2,1)} %param.6, f32[256,24,512]{2,1,0:T(8,128)} %get-tuple-element.8, f32[256,24]{1,0:T(8,128)S(1)} %get-tuple-element.7, s32[256,24]{1,0:T(8,128)S(1)} %broadcast_add_fusion, s32[512]{0:T(512)S(1)} %iota_add_fusion), kind=kOutput, calls=%fused_computation.12 | convolution fusion | flops 822607872 | bytes 47785984 | tf_op jit(solution)/shard_map/brs,bsd->brd/dot_general | solution.py:26
  85.9 1.5 %copy.16 = bf16[256,24,128]{2,0,1:T(8,128)(2,1)} copy(bf16[256,24,128]{2,1,0:T(8,128)(2,1)S(1)} %divide_convert_fusion) | data formatting | bytes 3145728 | tf_op jit(solution)/shard_map/convert_element_type | solution.py:27
  87.4 0.0 all-to-all-done
  87.4 4.6 %all-to-all-start.1 = ((bf16[256,8,3,128]{3,0,2,1:T(8,128)(2,1)}), bf16[256,8,3,128]{3,0,2,1:T(8,128)(2,1)S(1)}, u32[]{:S(2)}, u32[]{:S(2)}) async-start(bf16[256,8,3,128]{3,0,2,1:T(8,128)(2,1)} %bitcast), calls=%async_computation.1 | async-start | bytes 3145728 | tf_op jit(solution)/shard_map/all_to_all | solution.py:29
  92.0 21.5 %all-to-all-done.1 = bf16[256,8,3,128]{3,0,2,1:T(8,128)(2,1)S(1)} async-done(((bf16[256,8,3,128]{3,0,2,1:T(8,128)(2,1)}), bf16[256,8,3,128]{3,0,2,1:T(8,128)(2,1)S(1)}, u32[]{:S(2)}, u32[]{:S(2)}) %all-to-all-start.1) | async-done | bytes 1572896 | tf_op jit(solution)/shard_map/all_to_all | solution.py:29
  113.5 1.0 multiply_reduce_fusion
  114.5 0.9 divide_convert_fusion.1
  (5 shorter events, 0.1 us)
Async XLA Ops:
  6.5 25.5 %all-gather.2.cloned.1.call-start = ((), (), s32[]{:S(2)}) async-start(), calls=%async_computation.2 | async-start | bytes 1769472 | tf_op jit(solution)/shard_map/all_gather | solution.py:16
  64.9 22.5 %all-to-all-start = ((f32[256,8,3]{0,2,1:T(4,128)}), f32[256,8,3]{0,2,1:T(4,128)S(1)}, u32[]{:S(2)}, u32[]{:S(2)}) async-start(f32[256,8,3]{0,2,1:T(4,128)} %add.55), calls=%async_computation | async-start | bytes 65536 | tf_op jit(solution)/shard_map/all_to_all | solution.py:30
  87.4 26.1 %all-to-all-start.1 = ((bf16[256,8,3,128]{3,0,2,1:T(8,128)(2,1)}), bf16[256,8,3,128]{3,0,2,1:T(8,128)(2,1)S(1)}, u32[]{:S(2)}, u32[]{:S(2)}) async-start(bf16[256,8,3,128]{3,0,2,1:T(8,128)(2,1)} %bitcast), calls=%async_computation.1 | async-start | bytes 3145728 | tf_op jit(solution)/shard_map/all_to_all | solution.py:29
Sparse Core Ops, SparseCore 0:
  8.9 23.0 all-gather.1
where the time goes:
time: 122 us
  waiting for transfers between devices  46.2 us (38%)
  matrix products  42.2 us (35%)
  between operations  13.5 us (11%)
  other arithmetic  9.94 us (8%)
  starting transfers between devices  8.11 us (7%)
  local copies, waits for them, and re-layouts  2.26 us (2%)
    dot_general x1, matrix products, group_step(): jnp.einsum('brd,bsd->brs', q_group, k_span, preferred_element_type=jnp.fl...  24.8 us
    all_gather x1, waiting for transfers between devices, group_step(): q_group = lax.all_gather(q_local, 'dup', axis=1, tiled=True)  23.9 us
    all_to_all x1, waiting for transfers between devices, group_step(): recv_out = lax.all_to_all(part_out, 'dup', 1, 1)  21.5 us
    dot_general x1, matrix products, group_step(): jnp.einsum('brs,bsd->brd', prob_vals.astype(jnp.bfloat16), v_span, prefer...  17.4 us
    reduce_sum x1, other arithmetic, group_step(): row_mass = jnp.sum(prob_vals, axis=2, keepdims=True)  7.24 us
    all_to_all x1, starting transfers between devices, group_step(): recv_out = lax.all_to_all(part_out, 'dup', 1, 1)  4.56 us
    all_to_all x1, starting transfers between devices, group_step(): recv_mass = lax.all_to_all(log_mass, 'dup', 1, 1)  3.55 us
  transfers between devices with their start and end apart: 3, of which 2 were waited for; matrix products, arithmetic and copies ran while one was open for 16% of the time, Pallas kernels for 0%

commit v1 on v0

v1 whole, which is shorter than its diff:
```python
import functools

import jax
import jax.numpy as jnp
from jax import lax
from jax.experimental import pallas as pl
from jax.experimental.pallas import tpu as pltpu
from jax.sharding import PartitionSpec as P

DRAFT = 4
NEG_BIG = -3e38
LOG2E = 1.4426950408889634
MESH = pl.DeviceIdType.MESH

CHUNK = 32
GROUP = 8
SLOTS = 20
PITCH = CHUNK + 4


def attend(q_ref, len_ref, k_hbm, v_hbm, o_ref,
           kbuf, vbuf, q_all, q_wide, pos_rel, part_o, part_l,
           pair_so, pair_sl, pair_ro, pair_rl,
           chip_so, chip_sl, chip_ro, chip_rl, keep_o, keep_l,
           k_sem, v_sem, qs_sem, qr_sem, ps_sem, pr_sem, cs_sem, cr_sem):
    own, num_batch, head_dim = q_ref.shape
    span = k_hbm.shape[1]
    rows = 8 * own
    half = 4 * own
    chunks = num_batch // CHUNK
    groups = num_batch // GROUP
    scale = (head_dim ** -0.5) * LOG2E

    me = lax.axis_index("dup")
    chip = me // 2
    core = me % 2
    turn = 1 - 2 * core
    partner = chip * 2 + (1 - core)
    ahead = ((chip + turn + 4) % 4) * 2 + core
    behind = ((chip - turn + 4) % 4) * 2 + core
    across = ((chip + 2) % 4) * 2 + core

    def cache_copies(group):
        slot = group % SLOTS
        part = pl.ds(group * GROUP, GROUP)
        return (pltpu.make_async_copy(k_hbm.at[part], kbuf.at[slot], k_sem.at[slot]),
                pltpu.make_async_copy(v_hbm.at[part], vbuf.at[slot], v_sem.at[slot]))

    def start_cache(group, carry=0):
        for copy in cache_copies(group):
            copy.start()
        return carry

    lax.fori_loop(0, min(SLOTS, groups), start_cache, 0)

    barrier = pltpu.get_barrier_semaphore()
    for peer in (partner, ahead, behind, across):
        pl.semaphore_signal(barrier, inc=1, device_id={"dup": peer}, device_id_type=MESH)

    def q_copy(kind, c):
        part = pl.ds(pl.multiple_of(c * CHUNK, CHUNK), CHUNK)
        src, dst, peer = (
            (q_ref.at[:, part], q_all.at[2, :, part], behind),
            (q_ref.at[:, part], q_all.at[1, :, part], ahead),
            (q_ref.at[:, part], q_all.at[4, :, part], partner),
            (q_all.at[1, :, part], q_all.at[3, :, part], ahead),
            (q_all.at[1, :, part], q_all.at[5, :, part], partner),
            (q_all.at[2, :, part], q_all.at[6, :, part], partner),
            (q_all.at[3, :, part], q_all.at[7, :, part], partner),
        )[kind]
        return pltpu.make_async_remote_copy(
            src_ref=src, dst_ref=dst, send_sem=qs_sem.at[kind, c], recv_sem=qr_sem.at[kind, c],
            device_id={"dup": peer}, device_id_type=MESH)

    def q_own(c):
        for kind in (0, 1, 2):
            q_copy(kind, c).start()

    def q_pass_near(c):
        q_copy(1, c).wait_recv()
        q_copy(3, c).start()
        q_copy(4, c).start()
        q_copy(0, c).wait_recv()
        q_copy(5, c).start()

    def q_pass_far(c):
        q_copy(3, c).wait_recv()
        q_copy(6, c).start()

    span_start = me * span
    chip_disp = (0, 4 - turn, 4 + turn, 2)
    pair_disp = (0, 4 + turn, 4 - turn, 2)
    row_id = lax.broadcasted_iota(jnp.int32, (rows, span), 0)
    token = jnp.zeros((rows, span), jnp.int32)
    for h in range(2):
        for s in range(4):
            disp = (chip_disp, pair_disp)[h][s]
            device = ((chip + disp) % 4) * 2 + (core if h == 0 else 1 - core)
            for i in range(own):
                token = jnp.where(row_id == h * half + s * own + i, (own * device + i) % DRAFT, token)
    pos_rel[...] = lax.broadcasted_iota(jnp.int32, (rows, span), 1) + span_start - token

    pl.semaphore_wait(barrier, 4)
    q_own(0)
    q_own(1)
    q_pass_near(0)
    q_pass_far(0)

    def widen_queries(c):
        part = pl.ds(pl.multiple_of(c * CHUNK, CHUNK), CHUNK)
        for kind in (2, 4, 5, 6):
            q_copy(kind, c).wait_recv()
        for s in range(8):
            for i in range(own):
                block = q_ref[i, part, :] if s == 0 else q_all[s, i, part, :]
                q_wide[pl.ds((s * own + i) * PITCH, CHUNK), :] = block.astype(jnp.float32)

    def attend_pair(c, slot, first, j):
        zeros = jnp.zeros((rows, head_dim), jnp.float32)
        q0 = q_wide[pl.ds(first + j, rows, stride=PITCH), :]
        q1 = q_wide[pl.ds(first + j + 1, rows, stride=PITCH), :]
        q2 = jnp.concatenate([jnp.concatenate([q0, zeros], 1), jnp.concatenate([zeros, q1], 1)], 0).astype(jnp.bfloat16)
        k2 = jnp.concatenate([kbuf[slot, j], kbuf[slot, j + 1]], 1)
        s = lax.dot_general(q2, k2, (((1,), (1,)), ((), ())), preferred_element_type=jnp.float32)
        rel = pos_rel[...]
        base = c * CHUNK + first + j
        s = jnp.concatenate([
            jnp.where(rel <= len_ref[base] - DRAFT, s[:rows], NEG_BIG),
            jnp.where(rel <= len_ref[base + 1] - DRAFT, s[rows:], NEG_BIG)], 0)
        peak = jnp.max(s, axis=1, keepdims=True)
        p = jnp.exp2((s - peak) * scale)
        mass = jnp.sum(p, axis=1, keepdims=True)
        v2 = jnp.concatenate([vbuf[slot, j], vbuf[slot, j + 1]], 1)
        o2 = jnp.dot(p.astype(jnp.bfloat16), v2, preferred_element_type=jnp.float32)
        inv = 1.0 / mass
        log_mass = jnp.broadcast_to(peak * scale + jnp.log2(mass), (2 * rows, head_dim))
        par = c % 2
        for n in range(2):
            o = o2[n * rows:(n + 1) * rows, n * head_dim:(n + 1) * head_dim] * inv[n * rows:(n + 1) * rows]
            at = pl.ds(first + j + n, rows, stride=PITCH)
            part_o.at[par][at, :] = o
            part_l.at[par][at, :] = log_mass[n * rows:(n + 1) * rows]

    lane = lax.broadcasted_iota(jnp.int32, (CHUNK, head_dim), 1)
    seq = lax.broadcasted_iota(jnp.int32, (CHUNK, head_dim), 0)

    def to_lanes(values):
        total = jnp.zeros((CHUNK, head_dim), jnp.float32)
        for i, value in enumerate(values):
            total = jnp.where(lane == seq + i * CHUNK, value, total)
        return jnp.sum(total, axis=0, keepdims=True)

    def from_lanes(line, i):
        return jnp.sum(jnp.where(lane == seq + i * CHUNK, line, 0.0), axis=1, keepdims=True)

    def pair_copies(c):
        return tuple(pltpu.make_async_remote_copy(
            src_ref=src.at[c], dst_ref=dst.at[c], send_sem=ps_sem.at[n, c], recv_sem=pr_sem.at[n, c],
            device_id={"dup": partner}, device_id_type=MESH) for n, (src, dst) in enumerate(((pair_so, pair_ro), (pair_sl, pair_rl))))

    def chip_copies(c):
        copies = []
        for s, (there, peer) in enumerate(((1, behind), (0, ahead), (2, across))):
            for n, (src, dst) in enumerate(((chip_so, chip_ro), (chip_sl, chip_rl))):
                copies.append(pltpu.make_async_remote_copy(
                    src_ref=src.at[c, s], dst_ref=dst.at[c, there],
                    send_sem=cs_sem.at[n, s, c], recv_sem=cr_sem.at[n, there, c],
                    device_id={"dup": peer}, device_id_type=MESH))
        return copies

    def chip_arrivals(c):
        return [pltpu.make_async_remote_copy(
            src_ref=(chip_so, chip_sl)[n].at[c, s], dst_ref=(chip_ro, chip_rl)[n].at[c, s],
            send_sem=cs_sem.at[n, s, c], recv_sem=cr_sem.at[n, s, c],
            device_id={"dup": partner}, device_id_type=MESH) for s in range(3) for n in range(2)]

    def slab(ref, par, row):
        return ref.at[par][pl.ds(row * PITCH, CHUNK), :]

    def give_partner(c):
        par = c % 2
        for s in range(4):
            for i in range(own):
                pair_so[c, s, i * CHUNK:(i + 1) * CHUNK, :] = slab(part_o, par, half + s * own + i).astype(jnp.bfloat16)
        for s in range(4):
            pair_sl[c, s] = to_lanes([slab(part_l, par, half + s * own + i) for i in range(own)])
        for copy in pair_copies(c):
            copy.start()

    def merge_chip(c):
        par = c % 2
        for copy in pair_copies(c):
            copy.wait_recv()
        for s in (3, 1, 2, 0):
            logs = []
            line = pair_rl[c, s]
            for i in range(own):
                mine = slab(part_l, par, s * own + i)
                theirs = from_lanes(line, i)
                top = jnp.maximum(mine, theirs)
                w_mine, w_theirs = jnp.exp2(mine - top), jnp.exp2(theirs - top)
                total = w_mine + w_theirs
                o = (w_mine * slab(part_o, par, s * own + i)
                     + w_theirs * pair_ro[c, s, i * CHUNK:(i + 1) * CHUNK, :].astype(jnp.float32)) / total
                log_total = top + jnp.log2(total)
                if s == 0:
                    keep_o[par, i] = o
                    keep_l[par, i] = log_total
                else:
                    chip_so[c, s - 1, i * CHUNK:(i + 1) * CHUNK, :] = o.astype(jnp.bfloat16)
                    logs.append(log_total)
            if s:
                chip_sl[c, s - 1] = to_lanes(logs)
        for copy in chip_copies(c):
            copy.start()

    def merge_group(c):
        par = c % 2
        for copy in chip_arrivals(c):
            copy.wait_recv()
        lines = [chip_rl[c, s] for s in range(3)]
        for i in range(own):
            logs = [keep_l[par, i]] + [from_lanes(line, i) for line in lines]
            top = functools.reduce(jnp.maximum, logs)
            weights = [jnp.exp2(log - top) for log in logs]
            total = functools.reduce(jnp.add, weights)
            merged = weights[0] * keep_o[par, i]
            for s in range(3):
                merged = merged + weights[s + 1] * chip_ro[c, s, i * CHUNK:(i + 1) * CHUNK, :].astype(jnp.float32)
            o_ref[i, pl.ds(pl.multiple_of(c * CHUNK, CHUNK), CHUNK), :] = (merged / total).astype(jnp.bfloat16)

    def chunk_step(c, carry):
        @pl.when(c + 2 < chunks)
        def _():
            q_own(c + 2)

        @pl.when(c + 1 < chunks)
        def _():
            q_pass_near(c + 1)

        widen_queries(c)

        def group_step(g, inner):
            group = c * (CHUNK // GROUP) + g
            slot = group % SLOTS
            for copy in cache_copies(group):
                copy.wait()
            for j in range(0, GROUP, 2):
                attend_pair(c, slot, g * GROUP, j)

            @pl.when(group + SLOTS < groups)
            def _():
                start_cache(group + SLOTS)
            return inner

        lax.fori_loop(0, CHUNK // GROUP, group_step, 0)

        @pl.when(c + 1 < chunks)
        def _():
            q_pass_far(c + 1)

        give_partner(c)

        @pl.when(c >= 2)
        def _():
            merge_group(c - 2)

        @pl.when(c >= 1)
        def _():
            merge_chip(c - 1)
        return carry

    lax.fori_loop(0, chunks, chunk_step, 0)
    merge_group(chunks - 2)
    merge_chip(chunks - 1)
    merge_group(chunks - 1)

    def drain(c, carry):
        for kind in range(7):
            q_copy(kind, c).wait_send()
        for copy in pair_copies(c) + tuple(chip_copies(c)):
            copy.wait_send()
        return carry

    lax.fori_loop(0, chunks, drain, 0)


def solution(mesh):
    def group_step(q_local, k_span, v_span, len_local):
        num_batch, own, head_dim = q_local.shape
        span = k_span.shape[1]
        chunks = num_batch // CHUNK
        rows = 8 * own
        vmem = functools.partial(pl.BlockSpec, memory_space=pltpu.VMEM)
        hbm = functools.partial(pl.BlockSpec, memory_space=pl.ANY)
        bf16, f32 = jnp.bfloat16, jnp.float32
        dma = pltpu.SemaphoreType.DMA
        out = pl.pallas_call(
            attend,
            out_shape=jax.ShapeDtypeStruct((own, num_batch, head_dim), bf16),
            in_specs=[vmem(), pl.BlockSpec(memory_space=pltpu.SMEM), hbm(), hbm()],
            out_specs=vmem(),
            scratch_shapes=[
                pltpu.VMEM((SLOTS, GROUP, span, head_dim), bf16),
                pltpu.VMEM((SLOTS, GROUP, span, head_dim), bf16),
                pltpu.VMEM((8, own, num_batch, head_dim), bf16),
                pltpu.VMEM((rows * PITCH, head_dim), f32),
                pltpu.VMEM((rows, span), jnp.int32),
                pltpu.VMEM((2, rows * PITCH, head_dim), f32),
                pltpu.VMEM((2, rows * PITCH, head_dim), f32),
                pltpu.VMEM((chunks, 4, own * CHUNK, head_dim), bf16),
                pltpu.VMEM((chunks, 4, 1, head_dim), f32),
                pltpu.VMEM((chunks, 4, own * CHUNK, head_dim), bf16),
                pltpu.VMEM((chunks, 4, 1, head_dim), f32),
                pltpu.VMEM((chunks, 3, own * CHUNK, head_dim), bf16),
                pltpu.VMEM((chunks, 3, 1, head_dim), f32),
                pltpu.VMEM((chunks, 3, own * CHUNK, head_dim), bf16),
                pltpu.VMEM((chunks, 3, 1, head_dim), f32),
                pltpu.VMEM((2, own, CHUNK, head_dim), f32),
                pltpu.VMEM((2, own, CHUNK, head_dim), f32),
                dma((SLOTS,)), dma((SLOTS,)),
                dma((7, chunks)), dma((7, chunks)),
                dma((2, chunks)), dma((2, chunks)),
                dma((2, 3, chunks)), dma((2, 3, chunks)),
            ],
            compiler_params=pltpu.CompilerParams(
                collective_id=0, has_side_effects=True, vmem_limit_bytes=60 * 1024 * 1024),
            cost_estimate=pl.CostEstimate(
                flops=4 * num_batch * rows * span * head_dim,
                bytes_accessed=4 * num_batch * span * head_dim,
                transcendentals=num_batch * rows * span),
        )(q_local.transpose(1, 0, 2), len_local, k_span, v_span)
        return out.transpose(1, 0, 2)

    return jax.shard_map(
        group_step, mesh=mesh,
        in_specs=(P("kv", "dup", None), P("kv", "dup", None), P("kv", "dup", None), P("kv")),
        out_specs=P("kv", "dup", None), check_vma=False)
```

time: 122 us -> 76.6 us (0.63)
  Pallas kernels: 0 us -> 74.9 us
  waiting for transfers between devices: 46.2 us -> 0 us
  matrix products: 42.2 us -> 0 us
  between operations: 13.5 us -> 0.01 us
  other arithmetic: 9.94 us -> 0 us
  starting transfers between devices: 8.11 us -> 0 us
    pallas_call x0 -> x1, Pallas kernels: none -> 74.9 us  [group_step(): pl.pallas_call(attend, out_shape=jax.ShapeDtypeStruct((own, num_batch, he...]
    dot_general x2 -> x0, matrix products: 42.2 us -> none  [the longest x1 24.8 us: group_step(): jnp.einsum('brd,bsd->brs', q_group, k_span, preferred_element_type=jnp.fl...]
    all_gather x1 -> x0, waiting for transfers between devices: 23.9 us -> none  [group_step(): q_group = lax.all_gather(q_local, 'dup', axis=1, tiled=True)]
    all_to_all x2 -> x0, waiting for transfers between devices: 21.5 us -> none  [the longest x1 21.5 us: group_step(): recv_out = lax.all_to_all(part_out, 'dup', 1, 1)]
    reduce_sum x3 -> x0, other arithmetic: 8.26 us -> none  [the longest x1 7.24 us: group_step(): row_mass = jnp.sum(prob_vals, axis=2, keepdims=True)]
    all_to_all x2 -> x0, starting transfers between devices: 8.11 us -> none  [the longest x1 4.56 us: group_step(): recv_out = lax.all_to_all(part_out, 'dup', 1, 1)]
    unnamed x0 -> x1, local copies, waits for them, and re-layouts: none -> 1.62 us
    convert_element_type x1 -> x0, local copies, waits for them, and re-layouts: 1.51 us -> none  [group_step(): (weighted / row_mass).astype(jnp.bfloat16)]
  transfers between devices with their start and end apart: 3 -> 0, of which waited for: 2 -> 0; matrix products, arithmetic and copies ran while one was open for 16% -> 0% of each run, Pallas kernels for 0% -> 0%
where the time goes in v1:
time: 76.6 us; the launch traced here: 76.5 us
  Pallas kernels  74.9 us (98%)
  local copies, waits for them, and re-layouts  1.62 us (2%)
    pallas_call x1, Pallas kernels, group_step(): pl.pallas_call(attend, out_shape=jax.ShapeDtypeStruct((own, num_batch, he...  74.9 us
    unnamed x1, local copies, waits for them, and re-layouts  1.62 us

profile of v1, /device:TPU:112, one launch (start us, length us, event | category | flops | bytes accessed | tf_op | source)
XLA Modules:
  0.0 76.5 jit_solution(14994591256537029193)
XLA Ops:
  0.0 74.9 %shard_map.46 = bf16[3,256,128]{2,1,0:T(8,128)(2,1)} custom-call(bf16[3,256,128]{2,1,0:T(8,128)(2,1)} %bitcast.3, s32[256]{0:T(256)} %len_ref.1, bf16[256,512,128]{2,1,0:T(8,128)(2,1)} %k_hbm.1, bf16[256,512,128]{2,1,0:T(8,128)(2,1)} %v_hbm.1), custom_call_target="tpu_custom_call" | custom-call | flops 1610612736 | bytes 67108864 | tf_op jit(solution)/shard_map/pallas_call | solution.py:298
  74.9 1.6 %copy.6 = bf16[256,3,128]{2,0,1:T(8,128)(2,1)} copy(bf16[256,3,128]{2,0,1:T(8,128)(2,1)} %bitcast.2) | data formatting | bytes 393216

commit v2 on v1

--- a/solution.py
+++ b/solution.py
@@ -12,7 +12,7 @@
 LOG2E = 1.4426950408889634
 MESH = pl.DeviceIdType.MESH
 
-CHUNK = 32
+CHUNK = 64
 GROUP = 8
 SLOTS = 20
 PITCH = CHUNK + 4
@@ -144,14 +144,11 @@
     lane = lax.broadcasted_iota(jnp.int32, (CHUNK, head_dim), 1)
     seq = lax.broadcasted_iota(jnp.int32, (CHUNK, head_dim), 0)
 
-    def to_lanes(values):
-        total = jnp.zeros((CHUNK, head_dim), jnp.float32)
-        for i, value in enumerate(values):
-            total = jnp.where(lane == seq + i * CHUNK, value, total)
-        return jnp.sum(total, axis=0, keepdims=True)
-
-    def from_lanes(line, i):
-        return jnp.sum(jnp.where(lane == seq + i * CHUNK, line, 0.0), axis=1, keepdims=True)
+    def to_lanes(value):
+        return jnp.sum(jnp.where(lane == seq, value, 0.0), axis=0, keepdims=True)
+
+    def from_lanes(line):
+        return jnp.sum(jnp.where(lane == seq, line, 0.0), axis=1, keepdims=True)
 
     def pair_copies(c):
         return tuple(pltpu.make_async_remote_copy(
@@ -183,7 +180,8 @@
             for i in range(own):
                 pair_so[c, s, i * CHUNK:(i + 1) * CHUNK, :] = slab(part_o, par, half + s * own + i).astype(jnp.bfloat16)
         for s in range(4):
-            pair_sl[c, s] = to_lanes([slab(part_l, par, half + s * own + i) for i in range(own)])
+            for i in range(own):
+                pair_sl[c, s, i:i + 1, :] = to_lanes(slab(part_l, par, half + s * own + i))
         for copy in pair_copies(c):
             copy.start()
 
@@ -192,11 +190,9 @@
         for copy in pair_copies(c):
             copy.wait_recv()
         for s in (3, 1, 2, 0):
-            logs = []
-            line = pair_rl[c, s]
             for i in range(own):
                 mine = slab(part_l, par, s * own + i)
-                theirs = from_lanes(line, i)
+                theirs = from_lanes(pair_rl[c, s, i:i + 1, :])
                 top = jnp.maximum(mine, theirs)
                 w_mine, w_theirs = jnp.exp2(mine - top), jnp.exp2(theirs - top)
                 total = w_mine + w_theirs
@@ -208,9 +204,7 @@
                     keep_l[par, i] = log_total
                 else:
                     chip_so[c, s - 1, i * CHUNK:(i + 1) * CHUNK, :] = o.astype(jnp.bfloat16)
-                    logs.append(log_total)
-            if s:
-                chip_sl[c, s - 1] = to_lanes(logs)
+                    chip_sl[c, s - 1, i:i + 1, :] = to_lanes(log_total)
         for copy in chip_copies(c):
             copy.start()
 
@@ -218,9 +212,8 @@
         par = c % 2
         for copy in chip_arrivals(c):
             copy.wait_recv()
-        lines = [chip_rl[c, s] for s in range(3)]
         for i in range(own):
-            logs = [keep_l[par, i]] + [from_lanes(line, i) for line in lines]
+            logs = [keep_l[par, i]] + [from_lanes(chip_rl[c, s, i:i + 1, :]) for s in range(3)]
             top = functools.reduce(jnp.maximum, logs)
             weights = [jnp.exp2(log - top) for log in logs]
             total = functools.reduce(jnp.add, weights)
@@ -309,13 +302,13 @@
                 pltpu.VMEM((2, rows * PITCH, head_dim), f32),
                 pltpu.VMEM((2, rows * PITCH, head_dim), f32),
                 pltpu.VMEM((chunks, 4, own * CHUNK, head_dim), bf16),
-                pltpu.VMEM((chunks, 4, 1, head_dim), f32),
+                pltpu.VMEM((chunks, 4, own, head_dim), f32),
                 pltpu.VMEM((chunks, 4, own * CHUNK, head_dim), bf16),
-                pltpu.VMEM((chunks, 4, 1, head_dim), f32),
+                pltpu.VMEM((chunks, 4, own, head_dim), f32),
                 pltpu.VMEM((chunks, 3, own * CHUNK, head_dim), bf16),
-                pltpu.VMEM((chunks, 3, 1, head_dim), f32),
+                pltpu.VMEM((chunks, 3, own, head_dim), f32),
                 pltpu.VMEM((chunks, 3, own * CHUNK, head_dim), bf16),
-                pltpu.VMEM((chunks, 3, 1, head_dim), f32),
+                pltpu.VMEM((chunks, 3, own, head_dim), f32),
                 pltpu.VMEM((2, own, CHUNK, head_dim), f32),
                 pltpu.VMEM((2, own, CHUNK, head_dim), f32),
                 dma((SLOTS,)), dma((SLOTS,)),

time: 76.6 us -> 74.5 us (0.973)
  Pallas kernels: 74.9 us -> 72.8 us
    pallas_call x1, Pallas kernels: 74.9 us -> 72.8 us  [group_step(): pl.pallas_call(attend, out_shape=jax.ShapeDtypeStruct((own, num_batch, he...]
where the time goes in v2:
time: 74.5 us; the launch traced here: 74.4 us
  Pallas kernels  72.8 us (98%)
  local copies, waits for them, and re-layouts  1.62 us (2%)
    pallas_call x1, Pallas kernels, group_step(): pl.pallas_call(attend, out_shape=jax.ShapeDtypeStruct((own, num_batch, he...  72.8 us
    unnamed x1, local copies, waits for them, and re-layouts  1.62 us

profile of v2, /device:TPU:112, one launch (start us, length us, event | category | flops | bytes accessed | tf_op | source)
XLA Modules:
  0.0 74.4 jit_solution(8943164730429222290)
XLA Ops:
  0.0 72.8 %shard_map.46 = bf16[3,256,128]{2,1,0:T(8,128)(2,1)} custom-call(bf16[3,256,128]{2,1,0:T(8,128)(2,1)} %bitcast.3, s32[256]{0:T(256)} %len_ref.1, bf16[256,512,128]{2,1,0:T(8,128)(2,1)} %k_hbm.1, bf16[256,512,128]{2,1,0:T(8,128)(2,1)} %v_hbm.1), custom_call_target="tpu_custom_call" | custom-call | flops 1610612736 | bytes 67108864 | tf_op jit(solution)/shard_map/pallas_call | solution.py:291
  72.8 1.6 %copy.6 = bf16[256,3,128]{2,0,1:T(8,128)(2,1)} copy(bf16[256,3,128]{2,0,1:T(8,128)(2,1)} %bitcast.2) | data formatting | bytes 393216

commit v3 on v2

--- a/solution.py
+++ b/solution.py
@@ -15,6 +15,7 @@
 CHUNK = 64
 GROUP = 8
 SLOTS = 20
+TIMES = (1, 1, 1)
 PITCH = CHUNK + 4
 
 
@@ -22,7 +23,7 @@
            kbuf, vbuf, q_all, q_wide, pos_rel, part_o, part_l,
            pair_so, pair_sl, pair_ro, pair_rl,
            chip_so, chip_sl, chip_ro, chip_rl, keep_o, keep_l,
-           k_sem, v_sem, qs_sem, qr_sem, ps_sem, pr_sem, cs_sem, cr_sem):
+           k_sem, v_sem, qs_sem, qr_sem, ps_sem, pr_sem, cs_sem, cr_sem, s_buf, p_buf, i_buf):
     own, num_batch, head_dim = q_ref.shape
     span = k_hbm.shape[1]
     rows = 8 * own
@@ -115,13 +116,16 @@
                 block = q_ref[i, part, :] if s == 0 else q_all[s, i, part, :]
                 q_wide[pl.ds((s * own + i) * PITCH, CHUNK), :] = block.astype(jnp.float32)
 
-    def attend_pair(c, slot, first, j):
+    def score_pair(c, slot, first, j):
         zeros = jnp.zeros((rows, head_dim), jnp.float32)
         q0 = q_wide[pl.ds(first + j, rows, stride=PITCH), :]
         q1 = q_wide[pl.ds(first + j + 1, rows, stride=PITCH), :]
         q2 = jnp.concatenate([jnp.concatenate([q0, zeros], 1), jnp.concatenate([zeros, q1], 1)], 0).astype(jnp.bfloat16)
         k2 = jnp.concatenate([kbuf[slot, j], kbuf[slot, j + 1]], 1)
-        s = lax.dot_general(q2, k2, (((1,), (1,)), ((), ())), preferred_element_type=jnp.float32)
+        s_buf[j // 2] = lax.dot_general(q2, k2, (((1,), (1,)), ((), ())), preferred_element_type=jnp.float32)
+
+    def soft_pair(c, slot, first, j):
+        s = s_buf[j // 2]
         rel = pos_rel[...]
         base = c * CHUNK + first + j
         s = jnp.concatenate([
@@ -130,16 +134,23 @@
         peak = jnp.max(s, axis=1, keepdims=True)
         p = jnp.exp2((s - peak) * scale)
         mass = jnp.sum(p, axis=1, keepdims=True)
+        p_buf[j // 2] = p.astype(jnp.bfloat16)
+        i_buf[j // 2] = jnp.broadcast_to(1.0 / mass, (2 * rows, head_dim))
+        log_mass = jnp.broadcast_to(peak * scale + jnp.log2(mass), (2 * rows, head_dim))
+        par = c % 2
+        for n in range(2):
+            at = pl.ds(first + j + n, rows, stride=PITCH)
+            part_l.at[par][at, :] = log_mass[n * rows:(n + 1) * rows]
+
+    def mix_pair(c, slot, first, j):
         v2 = jnp.concatenate([vbuf[slot, j], vbuf[slot, j + 1]], 1)
-        o2 = jnp.dot(p.astype(jnp.bfloat16), v2, preferred_element_type=jnp.float32)
-        inv = 1.0 / mass
-        log_mass = jnp.broadcast_to(peak * scale + jnp.log2(mass), (2 * rows, head_dim))
+        o2 = jnp.dot(p_buf[j // 2], v2, preferred_element_type=jnp.float32)
+        inv = i_buf[j // 2]
         par = c % 2
         for n in range(2):
             o = o2[n * rows:(n + 1) * rows, n * head_dim:(n + 1) * head_dim] * inv[n * rows:(n + 1) * rows]
             at = pl.ds(first + j + n, rows, stride=PITCH)
             part_o.at[par][at, :] = o
-            part_l.at[par][at, :] = log_mass[n * rows:(n + 1) * rows]
 
     lane = lax.broadcasted_iota(jnp.int32, (CHUNK, head_dim), 1)
     seq = lax.broadcasted_iota(jnp.int32, (CHUNK, head_dim), 0)
@@ -238,8 +249,12 @@
             slot = group % SLOTS
             for copy in cache_copies(group):
                 copy.wait()
-            for j in range(0, GROUP, 2):
-                attend_pair(c, slot, g * GROUP, j)
+            for phase, times in ((score_pair, TIMES[0]), (soft_pair, TIMES[1]), (mix_pair, TIMES[2])):
+                def again(_, x):
+                    for j in range(0, GROUP, 2):
+                        phase(c, slot, g * GROUP, j)
+                    return x
+                lax.fori_loop(0, times, again, 0)
 
             @pl.when(group + SLOTS < groups)
             def _():
@@ -315,6 +330,7 @@
                 dma((7, chunks)), dma((7, chunks)),
                 dma((2, chunks)), dma((2, chunks)),
                 dma((2, 3, chunks)), dma((2, 3, chunks)),
+                pltpu.VMEM((GROUP // 2, 2 * rows, span), f32), pltpu.VMEM((GROUP // 2, 2 * rows, span), bf16), pltpu.VMEM((GROUP // 2, 2 * rows, head_dim), f32),
             ],
             compiler_params=pltpu.CompilerParams(
                 collective_id=0, has_side_effects=True, vmem_limit_bytes=60 * 1024 * 1024),

time: 74.5 us -> 53 us (0.71)
  Pallas kernels: 72.8 us -> 51.3 us
    pallas_call x1, Pallas kernels: 72.8 us -> 51.3 us  [group_step(): pl.pallas_call(attend, out_shape=jax.ShapeDtypeStruct((own, num_batch, he...]
where the time goes in v3:
time: 53 us; the launch traced here: 52.9 us
  Pallas kernels  51.3 us (97%)
  local copies, waits for them, and re-layouts  1.62 us (3%)
    pallas_call x1, Pallas kernels, group_step(): pl.pallas_call(attend, out_shape=jax.ShapeDtypeStruct((own, num_batch, he...  51.3 us
    unnamed x1, local copies, waits for them, and re-layouts  1.62 us

profile of v3, /device:TPU:112, one launch (start us, length us, event | category | flops | bytes accessed | tf_op | source)
XLA Modules:
  0.0 52.9 jit_solution(6296884040499880708)
XLA Ops:
  0.0 51.3 %shard_map.46 = bf16[3,256,128]{2,1,0:T(8,128)(2,1)} custom-call(bf16[3,256,128]{2,1,0:T(8,128)(2,1)} %bitcast.3, s32[256]{0:T(256)} %len_ref.1, bf16[256,512,128]{2,1,0:T(8,128)(2,1)} %k_hbm.1, bf16[256,512,128]{2,1,0:T(8,128)(2,1)} %v_hbm.1), custom_call_target="tpu_custom_call" | custom-call | flops 1610612736 | bytes 67108864 | tf_op jit(solution)/shard_map/pallas_call | solution.py:306
  51.3 1.6 %copy.6 = bf16[256,3,128]{2,0,1:T(8,128)(2,1)} copy(bf16[256,3,128]{2,0,1:T(8,128)(2,1)} %bitcast.2) | data formatting | bytes 393216

commit v4 on v1

v4 whole, which is shorter than its diff:
```python
import functools

import jax
import jax.numpy as jnp
from jax import lax
from jax.experimental import pallas as pl
from jax.experimental.pallas import tpu as pltpu
from jax.sharding import PartitionSpec as P

DRAFT = 4
NEG_BIG = -3e38
LOG2E = 1.4426950408889634
MESH = pl.DeviceIdType.MESH

GROUP = 16
KEYS = 10
VALUES = 11
PITCH = GROUP + 4
RING = 8
KEEP = 16
ASK = 2
GIVE, MERGE, FINAL = 3, 5, 9


def attend(q_ref, len_ref, k_hbm, v_hbm, o_ref,
           kbuf, vbuf, q_all, q_wide, pos_rel, s_buf, p_buf, i_buf, part_o, part_l,
           pair_so, pair_sl, pair_ro, pair_rl,
           chip_so, chip_sl, chip_ro, chip_rl, keep_o, keep_l,
           k_sem, v_sem, qs_sem, qr_sem, ps_sem, pr_sem, cs_sem, cr_sem):
    own, num_batch, head_dim = q_ref.shape
    span = k_hbm.shape[1]
    rows = 8 * own
    half = 4 * own
    steps = num_batch // GROUP
    asks = steps // ASK
    scale = (head_dim ** -0.5) * LOG2E

    me = lax.axis_index("dup")
    chip = me // 2
    core = me % 2
    turn = 1 - 2 * core
    partner = chip * 2 + (1 - core)
    ahead = ((chip + turn + 4) % 4) * 2 + core
    behind = ((chip - turn + 4) % 4) * 2 + core
    across = ((chip + 2) % 4) * 2 + core

    def key_copy(g):
        return pltpu.make_async_copy(k_hbm.at[pl.ds(g * GROUP, GROUP)], kbuf.at[g % KEYS], k_sem.at[g % KEYS])

    def value_copy(g):
        return pltpu.make_async_copy(v_hbm.at[pl.ds(g * GROUP, GROUP)], vbuf.at[g % VALUES], v_sem.at[g % VALUES])

    key_copy(0).start()
    key_copy(1).start()

    def start_cache(g, carry):
        key_copy(g + 2).start()
        value_copy(g).start()
        return carry

    lax.fori_loop(0, KEYS - 2, start_cache, 0)
    for g in range(KEYS - 2, VALUES):
        value_copy(g).start()

    barrier = pltpu.get_barrier_semaphore()
    for peer in (partner, ahead, behind, across):
        pl.semaphore_signal(barrier, inc=1, device_id={"dup": peer}, device_id_type=MESH)

    def q_copy(kind, c):
        part = pl.ds(pl.multiple_of(c * ASK * GROUP, ASK * GROUP), ASK * GROUP)
        src, dst, peer = (
            (q_ref.at[:, part], q_all.at[2, :, part], behind),
            (q_ref.at[:, part], q_all.at[1, :, part], ahead),
            (q_ref.at[:, part], q_all.at[4, :, part], partner),
            (q_all.at[1, :, part], q_all.at[3, :, part], ahead),
            (q_all.at[1, :, part], q_all.at[5, :, part], partner),
            (q_all.at[2, :, part], q_all.at[6, :, part], partner),
            (q_all.at[3, :, part], q_all.at[7, :, part], partner),
        )[kind]
        return pltpu.make_async_remote_copy(
            src_ref=src, dst_ref=dst, send_sem=qs_sem.at[kind, c], recv_sem=qr_sem.at[kind, c],
            device_id={"dup": peer}, device_id_type=MESH)

    def q_own(c):
        for kind in (0, 1, 2):
            q_copy(kind, c).start()

    def q_pass_near(c):
        q_copy(1, c).wait_recv()
        q_copy(3, c).start()
        q_copy(4, c).start()
        q_copy(0, c).wait_recv()
        q_copy(5, c).start()

    def q_pass_far(c):
        q_copy(3, c).wait_recv()
        q_copy(6, c).start()

    span_start = me * span
    chip_disp = (0, 4 - turn, 4 + turn, 2)
    pair_disp = (0, 4 + turn, 4 - turn, 2)
    row_id = lax.broadcasted_iota(jnp.int32, (rows, span), 0)
    token = jnp.zeros((rows, span), jnp.int32)
    for h in range(2):
        for s in range(4):
            disp = (chip_disp, pair_disp)[h][s]
            device = ((chip + disp) % 4) * 2 + (core if h == 0 else 1 - core)
            for i in range(own):
                token = jnp.where(row_id == h * half + s * own + i, (own * device + i) % DRAFT, token)
    pos_rel[...] = lax.broadcasted_iota(jnp.int32, (rows, span), 1) + span_start - token

    pl.semaphore_wait(barrier, 4)
    q_own(0)
    q_own(1)
    q_pass_near(0)
    q_pass_far(0)
    q_pass_near(1)
    q_own(2)
    q_own(3)

    def q_arrive(c):
        for kind in (2, 4, 5, 6):
            q_copy(kind, c).wait_recv()

    lane = lax.broadcasted_iota(jnp.int32, (GROUP, head_dim), 1)
    seq = lax.broadcasted_iota(jnp.int32, (GROUP, head_dim), 0)

    def score(g):
        part = pl.ds(pl.multiple_of(g * GROUP, GROUP), GROUP)
        for s in range(8):
            for i in range(own):
                block = q_ref[i, part, :] if s == 0 else q_all[s, i, part, :]
                q_wide[pl.ds((s * own + i) * PITCH, GROUP), :] = block.astype(jnp.float32)
        slot = g % KEYS
        zeros = jnp.zeros((rows, head_dim), jnp.float32)
        for j in range(0, GROUP, 2):
            q0 = q_wide[pl.ds(j, rows, stride=PITCH), :]
            q1 = q_wide[pl.ds(j + 1, rows, stride=PITCH), :]
            q2 = jnp.concatenate([jnp.concatenate([q0, zeros], 1), jnp.concatenate([zeros, q1], 1)], 0).astype(jnp.bfloat16)
            k2 = jnp.concatenate([kbuf[slot, j], kbuf[slot, j + 1]], 1)
            s_buf[j // 2] = lax.dot_general(q2, k2, (((1,), (1,)), ((), ())), preferred_element_type=jnp.float32)

    def soften(g):
        slab_l = part_l.at[g % RING]
        for j in range(0, GROUP, 2):
            s = s_buf[j // 2]
            rel = pos_rel[...]
            base = g * GROUP + j
            s = jnp.concatenate([
                jnp.where(rel <= len_ref[base] - DRAFT, s[:rows], NEG_BIG),
                jnp.where(rel <= len_ref[base + 1] - DRAFT, s[rows:], NEG_BIG)], 0)
            peak = jnp.max(s, axis=1, keepdims=True)
            p = jnp.exp2((s - peak) * scale)
            mass = jnp.sum(p, axis=1, keepdims=True)
            p_buf[j // 2] = p.astype(jnp.bfloat16)
            i_buf[j // 2] = jnp.broadcast_to(1.0 / mass, (2 * rows, head_dim))
            log_mass = jnp.broadcast_to(peak * scale + jnp.log2(mass), (2 * rows, head_dim))
            for n in range(2):
                slab_l[pl.ds(j + n, rows, stride=PITCH), :] = log_mass[n * rows:(n + 1) * rows]

    def mix(g):
        slot = g % VALUES
        slab_o = part_o.at[g % RING]
        for j in range(0, GROUP, 2):
            v2 = jnp.concatenate([vbuf[slot, j], vbuf[slot, j + 1]], 1)
            o2 = jnp.dot(p_buf[j // 2], v2, preferred_element_type=jnp.float32)
            inv = i_buf[j // 2]
            for n in range(2):
                o = o2[n * rows:(n + 1) * rows, n * head_dim:(n + 1) * head_dim] * inv[n * rows:(n + 1) * rows]
                slab_o[pl.ds(j + n, rows, stride=PITCH), :] = o

    def to_lanes(values):
        total = jnp.zeros((GROUP, head_dim), jnp.float32)
        for i, value in enumerate(values):
            total = jnp.where(lane == seq + i * GROUP, value, total)
        return jnp.sum(total, axis=0, keepdims=True)

    def from_lanes(line, i):
        return jnp.sum(jnp.where(lane == seq + i * GROUP, line, 0.0), axis=1, keepdims=True)

    def pair_copies(c):
        return tuple(pltpu.make_async_remote_copy(
            src_ref=src.at[c], dst_ref=dst.at[c], send_sem=ps_sem.at[n, c], recv_sem=pr_sem.at[n, c],
            device_id={"dup": partner}, device_id_type=MESH) for n, (src, dst) in enumerate(((pair_so, pair_ro), (pair_sl, pair_rl))))

    def chip_copies(c):
        copies = []
        for s, (there, peer) in enumerate(((1, behind), (0, ahead), (2, across))):
            for n, (src, dst) in enumerate(((chip_so, chip_ro), (chip_sl, chip_rl))):
                copies.append(pltpu.make_async_remote_copy(
                    src_ref=src.at[c, s], dst_ref=dst.at[c, there],
                    send_sem=cs_sem.at[n, s, c], recv_sem=cr_sem.at[n, there, c],
                    device_id={"dup": peer}, device_id_type=MESH))
        return copies

    def chip_arrivals(c):
        return [pltpu.make_async_remote_copy(
            src_ref=(chip_so, chip_sl)[n].at[c, s], dst_ref=(chip_ro, chip_rl)[n].at[c, s],
            send_sem=cs_sem.at[n, s, c], recv_sem=cr_sem.at[n, s, c],
            device_id={"dup": partner}, device_id_type=MESH) for s in range(3) for n in range(2)]

    def slab(ref, g, row):
        return ref.at[g % RING][pl.ds(row * PITCH, GROUP), :]

    spare = FINAL

    def place(g):
        return (g + steps + spare) % (steps + spare)

    def give(g):
        c, r = place(g), g + KEEP
        for s in range(4):
            for i in range(own):
                pair_so[c, s, i * GROUP:(i + 1) * GROUP, :] = slab(part_o, r, half + s * own + i).astype(jnp.bfloat16)
        for s in range(4):
            pair_sl[c, s] = to_lanes([slab(part_l, r, half + s * own + i) for i in range(own)])

    def merge(g):
        c, r = place(g), g + KEEP
        for s in (3, 1, 2, 0):
            logs = []
            line = pair_rl[c, s]
            for i in range(own):
                mine = slab(part_l, r, s * own + i)
                theirs = from_lanes(line, i)
                top = jnp.maximum(mine, theirs)
                w_mine, w_theirs = jnp.exp2(mine - top), jnp.exp2(theirs - top)
                total = w_mine + w_theirs
                o = (w_mine * slab(part_o, r, s * own + i)
                     + w_theirs * pair_ro[c, s, i * GROUP:(i + 1) * GROUP, :].astype(jnp.float32)) / total
                log_total = top + jnp.log2(total)
                if s == 0:
                    keep_o[r % KEEP, i] = o
                    keep_l[r % KEEP, i] = log_total
                else:
                    chip_so[c, s - 1, i * GROUP:(i + 1) * GROUP, :] = o.astype(jnp.bfloat16)
                    logs.append(log_total)
            if s:
                chip_sl[c, s - 1] = to_lanes(logs)

    def final(g):
        c, r = place(g), g + KEEP
        to = pl.ds(pl.multiple_of(((g + steps) % steps) * GROUP, GROUP), GROUP)
        lines = [chip_rl[c, s] for s in range(3)]
        for i in range(own):
            logs = [keep_l[r % KEEP, i]] + [from_lanes(line, i) for line in lines]
            top = functools.reduce(jnp.maximum, logs)
            weights = [jnp.exp2(log - top) for log in logs]
            total = functools.reduce(jnp.add, weights)
            merged = weights[0] * keep_o[r % KEEP, i]
            for s in range(3):
                merged = merged + weights[s + 1] * chip_ro[c, s, i * GROUP:(i + 1) * GROUP, :].astype(jnp.float32)
            o_ref[i, to, :] = (merged / total).astype(jnp.bfloat16)

    def start_all(copies):
        for copy in copies:
            copy.start()

    def arrive_all(copies):
        for copy in copies:
            copy.wait_recv()

    q_arrive(0)
    key_copy(0).wait()
    score(0)
    key_copy(KEYS).start()
    key_copy(1).wait()
    soften(0)
    score(1)
    key_copy(KEYS + 1).start()
    q_pass_far(1)
    q_pass_near(2)

    def step(t, carry):
        c = t // ASK

        @pl.when(t % ASK == 0)
        def _():
            @pl.when(c + 3 < asks)
            def _():
                q_own(c + 3)

            @pl.when(c + 2 < asks)
            def _():
                q_pass_near(c + 2)

            @pl.when(c + 1 < asks)
            def _():
                q_pass_far(c + 1)

            q_arrive(c)

        key_copy(t).wait()
        value_copy(t - 2).wait()

        @pl.when(t >= MERGE)
        def _():
            arrive_all(pair_copies(t - MERGE))

        @pl.when(t >= FINAL)
        def _():
            arrive_all(chip_arrivals(t - FINAL))

        final(t - FINAL)
        merge(t - MERGE)
        give(t - GIVE)
        mix(t - 2)
        soften(t - 1)
        score(t)

        @pl.when(t + KEYS < steps)
        def _():
            key_copy(t + KEYS).start()

        @pl.when(t - 2 + VALUES < steps)
        def _():
            value_copy(t - 2 + VALUES).start()

        @pl.when(t >= GIVE)
        def _():
            start_all(pair_copies(t - GIVE))

        @pl.when(t >= MERGE)
        def _():
            start_all(chip_copies(t - MERGE))
        return carry

    lax.fori_loop(2, steps, step, 0)

    value_copy(steps - 2).wait()
    value_copy(steps - 1).wait()
    give(steps - GIVE)
    mix(steps - 2)
    soften(steps - 1)
    start_all(pair_copies(steps - GIVE))
    give(steps - 2)
    mix(steps - 1)
    start_all(pair_copies(steps - 2))
    give(steps - 1)
    start_all(pair_copies(steps - 1))

    def last_merge(g, carry):
        arrive_all(pair_copies(g))
        merge(g)
        start_all(chip_copies(g))
        return carry

    lax.fori_loop(steps - MERGE, steps, last_merge, 0)

    def last_final(g, carry):
        arrive_all(chip_arrivals(g))
        final(g)
        return carry

    lax.fori_loop(steps - FINAL, steps, last_final, 0)

    def drain_asks(c, carry):
        for kind in range(7):
            q_copy(kind, c).wait_send()
        return carry

    lax.fori_loop(0, asks, drain_asks, 0)

    def drain(c, carry):
        for copy in pair_copies(c) + tuple(chip_copies(c)):
            copy.wait_send()
        return carry

    lax.fori_loop(0, steps, drain, 0)


def solution(mesh):
    def group_step(q_local, k_span, v_span, len_local):
        num_batch, own, head_dim = q_local.shape
        span = k_span.shape[1]
        steps = num_batch // GROUP
        asks = steps // ASK
        places = steps + FINAL
        rows = 8 * own
        vmem = functools.partial(pl.BlockSpec, memory_space=pltpu.VMEM)
        hbm = functools.partial(pl.BlockSpec, memory_space=pl.ANY)
        bf16, f32 = jnp.bfloat16, jnp.float32
        dma = pltpu.SemaphoreType.DMA
        out = pl.pallas_call(
            attend,
            out_shape=jax.ShapeDtypeStruct((own, num_batch, head_dim), bf16),
            in_specs=[vmem(), pl.BlockSpec(memory_space=pltpu.SMEM), hbm(), hbm()],
            out_specs=vmem(),
            scratch_shapes=[
                pltpu.VMEM((KEYS, GROUP, span, head_dim), bf16),
                pltpu.VMEM((VALUES, GROUP, span, head_dim), bf16),
                pltpu.VMEM((8, own, num_batch, head_dim), bf16),
                pltpu.VMEM((rows * PITCH, head_dim), f32),
                pltpu.VMEM((rows, span), jnp.int32),
                pltpu.VMEM((GROUP // 2, 2 * rows, span), f32),
                pltpu.VMEM((GROUP // 2, 2 * rows, span), bf16),
                pltpu.VMEM((GROUP // 2, 2 * rows, head_dim), f32),
                pltpu.VMEM((RING, rows * PITCH, head_dim), f32),
                pltpu.VMEM((RING, rows * PITCH, head_dim), f32),
                pltpu.VMEM((places, 4, own * GROUP, head_dim), bf16),
                pltpu.VMEM((places, 4, 1, head_dim), f32),
                pltpu.VMEM((places, 4, own * GROUP, head_dim), bf16),
                pltpu.VMEM((places, 4, 1, head_dim), f32),
                pltpu.VMEM((places, 3, own * GROUP, head_dim), bf16),
                pltpu.VMEM((places, 3, 1, head_dim), f32),
                pltpu.VMEM((places, 3, own * GROUP, head_dim), bf16),
                pltpu.VMEM((places, 3, 1, head_dim), f32),
                pltpu.VMEM((KEEP, own, GROUP, head_dim), f32),
                pltpu.VMEM((KEEP, own, GROUP, head_dim), f32),
                dma((KEYS,)), dma((VALUES,)),
                dma((7, asks)), dma((7, asks)),
                dma((2, steps)), dma((2, steps)),
                dma((2, 3, steps)), dma((2, 3, steps)),
            ],
            compiler_params=pltpu.CompilerParams(
                collective_id=0, has_side_effects=True, vmem_limit_bytes=60 * 1024 * 1024),
            cost_estimate=pl.CostEstimate(
                flops=4 * num_batch * rows * span * head_dim,
                bytes_accessed=4 * num_batch * span * head_dim,
                transcendentals=num_batch * rows * span),
        )(q_local.transpose(1, 0, 2), len_local, k_span, v_span)
        return out.transpose(1, 0, 2)

    return jax.shard_map(
        group_step, mesh=mesh,
        in_specs=(P("kv", "dup", None), P("kv", "dup", None), P("kv", "dup", None), P("kv")),
        out_specs=P("kv", "dup", None), check_vma=False)
```

time: 76.6 us -> 50.5 us (0.66)
  Pallas kernels: 74.9 us -> 48.8 us
    pallas_call x1, Pallas kernels: 74.9 us -> 48.8 us  [group_step(): pl.pallas_call(attend, out_shape=jax.ShapeDtypeStruct((own, num_batch, he...]
where the time goes in v4:
time: 50.5 us; the launch traced here: 50.4 us
  Pallas kernels  48.8 us (97%)
  local copies, waits for them, and re-layouts  1.62 us (3%)
    pallas_call x1, Pallas kernels, group_step(): pl.pallas_call(attend, out_shape=jax.ShapeDtypeStruct((own, num_batch, he...  48.8 us
    unnamed x1, local copies, waits for them, and re-layouts  1.62 us

profile of v4, /device:TPU:112, one launch (start us, length us, event | category | flops | bytes accessed | tf_op | source)
XLA Modules:
  0.0 50.4 jit_solution(9365477412096787822)
XLA Ops:
  0.0 48.8 %shard_map.46 = bf16[3,256,128]{2,1,0:T(8,128)(2,1)} custom-call(bf16[3,256,128]{2,1,0:T(8,128)(2,1)} %bitcast.3, s32[256]{0:T(256)} %len_ref.1, bf16[256,512,128]{2,1,0:T(8,128)(2,1)} %k_hbm.1, bf16[256,512,128]{2,1,0:T(8,128)(2,1)} %v_hbm.1), custom_call_target="tpu_custom_call" | custom-call | flops 1610612736 | bytes 67108864 | tf_op jit(solution)/shard_map/pallas_call | solution.py:384
  48.8 1.6 %copy.6 = bf16[256,3,128]{2,0,1:T(8,128)(2,1)} copy(bf16[256,3,128]{2,0,1:T(8,128)(2,1)} %bitcast.2) | data formatting | bytes 393216

commit v5 on v4

--- a/solution.py
+++ b/solution.py
@@ -19,14 +19,14 @@
 RING = 8
 KEEP = 16
 ASK = 2
-GIVE, MERGE, FINAL = 3, 5, 9
+GIVE, MERGE, RELAY, FINAL = 3, 5, 7, 9
 
 
 def attend(q_ref, len_ref, k_hbm, v_hbm, o_ref,
            kbuf, vbuf, q_all, q_wide, pos_rel, s_buf, p_buf, i_buf, part_o, part_l,
            pair_so, pair_sl, pair_ro, pair_rl,
-           chip_so, chip_sl, chip_ro, chip_rl, keep_o, keep_l,
-           k_sem, v_sem, qs_sem, qr_sem, ps_sem, pr_sem, cs_sem, cr_sem):
+           chip_so, chip_sl, chip_ro, chip_rl, relay_o, relay_l, keep_o, keep_l,
+           k_sem, v_sem, qs_sem, qr_sem, ps_sem, pr_sem, cs_sem, cr_sem, rs_sem, rr_sem):
     own, num_batch, head_dim = q_ref.shape
     span = k_hbm.shape[1]
     rows = 8 * own
@@ -42,7 +42,6 @@
     partner = chip * 2 + (1 - core)
     ahead = ((chip + turn + 4) % 4) * 2 + core
     behind = ((chip - turn + 4) % 4) * 2 + core
-    across = ((chip + 2) % 4) * 2 + core
 
     def key_copy(g):
         return pltpu.make_async_copy(k_hbm.at[pl.ds(g * GROUP, GROUP)], kbuf.at[g % KEYS], k_sem.at[g % KEYS])
@@ -63,7 +62,7 @@
         value_copy(g).start()
 
     barrier = pltpu.get_barrier_semaphore()
-    for peer in (partner, ahead, behind, across):
+    for peer in (partner, ahead, behind):
         pl.semaphore_signal(barrier, inc=1, device_id={"dup": peer}, device_id_type=MESH)
 
     def q_copy(kind, c):
@@ -109,7 +108,7 @@
                 token = jnp.where(row_id == h * half + s * own + i, (own * device + i) % DRAFT, token)
     pos_rel[...] = lax.broadcasted_iota(jnp.int32, (rows, span), 1) + span_start - token
 
-    pl.semaphore_wait(barrier, 4)
+    pl.semaphore_wait(barrier, 3)
     q_own(0)
     q_own(1)
     q_pass_near(0)
@@ -185,13 +184,27 @@
 
     def chip_copies(c):
         copies = []
-        for s, (there, peer) in enumerate(((1, behind), (0, ahead), (2, across))):
-            for n, (src, dst) in enumerate(((chip_so, chip_ro), (chip_sl, chip_rl))):
+        for n, (src, dst, via) in enumerate(((chip_so, chip_ro, relay_o), (chip_sl, chip_rl, relay_l))):
+            for s, to, sem, peer in ((2, via.at[c], rr_sem.at[n, c], ahead),
+                                     (1, dst.at[c, 0], cr_sem.at[n, 0, c], ahead),
+                                     (0, dst.at[c, 1], cr_sem.at[n, 1, c], behind)):
                 copies.append(pltpu.make_async_remote_copy(
-                    src_ref=src.at[c, s], dst_ref=dst.at[c, there],
-                    send_sem=cs_sem.at[n, s, c], recv_sem=cr_sem.at[n, there, c],
+                    src_ref=src.at[c, s], dst_ref=to, send_sem=cs_sem.at[n, s, c], recv_sem=sem,
                     device_id={"dup": peer}, device_id_type=MESH))
         return copies
+
+    def relay_copies(c):
+        return [pltpu.make_async_remote_copy(
+            src_ref=via.at[c], dst_ref=dst.at[c, 2], send_sem=rs_sem.at[n, c], recv_sem=cr_sem.at[n, 2, c],
+            device_id={"dup": ahead}, device_id_type=MESH) for n, (via, dst) in enumerate(((relay_o, chip_ro), (relay_l, chip_rl)))]
+
+    def pass_on(c):
+        for n, via in enumerate((relay_o, relay_l)):
+            pltpu.make_async_remote_copy(
+                src_ref=via.at[c], dst_ref=via.at[c], send_sem=rs_sem.at[n, c], recv_sem=rr_sem.at[n, c],
+                device_id={"dup": ahead}, device_id_type=MESH).wait_recv()
+        for copy in relay_copies(c):
+            copy.start()
 
     def chip_arrivals(c):
         return [pltpu.make_async_remote_copy(
@@ -297,6 +310,10 @@
         def _():
             arrive_all(pair_copies(t - MERGE))
 
+        @pl.when(t >= RELAY)
+        def _():
+            pass_on(t - RELAY)
+
         @pl.when(t >= FINAL)
         def _():
             arrive_all(chip_arrivals(t - FINAL))
@@ -343,16 +360,19 @@
         arrive_all(pair_copies(g))
         merge(g)
         start_all(chip_copies(g))
-        return carry
-
-    lax.fori_loop(steps - MERGE, steps, last_merge, 0)
+        pass_on(g - 2)
+        return carry
 
     def last_final(g, carry):
         arrive_all(chip_arrivals(g))
         final(g)
         return carry
 
-    lax.fori_loop(steps - FINAL, steps, last_final, 0)
+    lax.fori_loop(steps - MERGE, steps, last_merge, 0)
+    lax.fori_loop(steps - FINAL, steps - 5, last_final, 0)
+    pass_on(steps - 2)
+    pass_on(steps - 1)
+    lax.fori_loop(steps - 5, steps, last_final, 0)
 
     def drain_asks(c, carry):
         for kind in range(7):
@@ -362,7 +382,7 @@
     lax.fori_loop(0, asks, drain_asks, 0)
 
     def drain(c, carry):
-        for copy in pair_copies(c) + tuple(chip_copies(c)):
+        for copy in list(pair_copies(c)) + chip_copies(c) + relay_copies(c):
             copy.wait_send()
         return carry
 
@@ -405,12 +425,15 @@
                 pltpu.VMEM((places, 3, 1, head_dim), f32),
                 pltpu.VMEM((places, 3, own * GROUP, head_dim), bf16),
                 pltpu.VMEM((places, 3, 1, head_dim), f32),
+                pltpu.VMEM((steps, own * GROUP, head_dim), bf16),
+                pltpu.VMEM((steps, 1, head_dim), f32),
                 pltpu.VMEM((KEEP, own, GROUP, head_dim), f32),
                 pltpu.VMEM((KEEP, own, GROUP, head_dim), f32),
                 dma((KEYS,)), dma((VALUES,)),
                 dma((7, asks)), dma((7, asks)),
                 dma((2, steps)), dma((2, steps)),
                 dma((2, 3, steps)), dma((2, 3, steps)),
+                dma((2, steps)), dma((2, steps)),
             ],
             compiler_params=pltpu.CompilerParams(
                 collective_id=0, has_side_effects=True, vmem_limit_bytes=60 * 1024 * 1024),

time: 50.5 us -> 61.2 us (1.21)
  Pallas kernels: 48.8 us -> 59.4 us
    pallas_call x1, Pallas kernels: 48.8 us -> 59.4 us  [group_step(): pl.pallas_call(attend, out_shape=jax.ShapeDtypeStruct((own, num_batch, he...]
where the time goes in v5:
time: 61.2 us; the launch traced here: 61.1 us
  Pallas kernels  59.4 us (97%)
  local copies, waits for them, and re-layouts  1.62 us (3%)
    pallas_call x1, Pallas kernels, group_step(): pl.pallas_call(attend, out_shape=jax.ShapeDtypeStruct((own, num_batch, he...  59.4 us
    unnamed x1, local copies, waits for them, and re-layouts  1.62 us

profile of v5, /device:TPU:112, one launch (start us, length us, event | category | flops | bytes accessed | tf_op | source)
XLA Modules:
  0.0 61.1 jit_solution(947271289340332352)
XLA Ops:
  0.0 59.4 %shard_map.46 = bf16[3,256,128]{2,1,0:T(8,128)(2,1)} custom-call(bf16[3,256,128]{2,1,0:T(8,128)(2,1)} %bitcast.3, s32[256]{0:T(256)} %len_ref.1, bf16[256,512,128]{2,1,0:T(8,128)(2,1)} %k_hbm.1, bf16[256,512,128]{2,1,0:T(8,128)(2,1)} %v_hbm.1), custom_call_target="tpu_custom_call" | custom-call | flops 1610612736 | bytes 67108864 | tf_op jit(solution)/shard_map/pallas_call | solution.py:404
  59.4 1.6 %copy.6 = bf16[256,3,128]{2,0,1:T(8,128)(2,1)} copy(bf16[256,3,128]{2,0,1:T(8,128)(2,1)} %bitcast.2) | data formatting | bytes 393216

commit v6 on v4

--- a/solution.py
+++ b/solution.py
@@ -19,18 +19,19 @@
 RING = 8
 KEEP = 16
 ASK = 2
-GIVE, MERGE, FINAL = 3, 5, 9
+GIVE, MERGE, FINAL = 3, 6, 12
+SPARE = 12
 
 
 def attend(q_ref, len_ref, k_hbm, v_hbm, o_ref,
            kbuf, vbuf, q_all, q_wide, pos_rel, s_buf, p_buf, i_buf, part_o, part_l,
-           pair_so, pair_sl, pair_ro, pair_rl,
-           chip_so, chip_sl, chip_ro, chip_rl, keep_o, keep_l,
+           pair_so, pair_ro, chip_so, chip_ro, pair_held, chip_held, keep_o, keep_l,
            k_sem, v_sem, qs_sem, qr_sem, ps_sem, pr_sem, cs_sem, cr_sem):
     own, num_batch, head_dim = q_ref.shape
     span = k_hbm.shape[1]
     rows = 8 * own
     half = 4 * own
+    data = 2 * own * GROUP
     steps = num_batch // GROUP
     asks = steps // ASK
     scale = (head_dim ** -0.5) * LOG2E
@@ -73,9 +74,7 @@
             (q_ref.at[:, part], q_all.at[1, :, part], ahead),
             (q_ref.at[:, part], q_all.at[4, :, part], partner),
             (q_all.at[1, :, part], q_all.at[3, :, part], ahead),
-            (q_all.at[1, :, part], q_all.at[5, :, part], partner),
-            (q_all.at[2, :, part], q_all.at[6, :, part], partner),
-            (q_all.at[3, :, part], q_all.at[7, :, part], partner),
+            (q_all.at[1:4, :, part], q_all.at[5:8, :, part], partner),
         )[kind]
         return pltpu.make_async_remote_copy(
             src_ref=src, dst_ref=dst, send_sem=qs_sem.at[kind, c], recv_sem=qr_sem.at[kind, c],
@@ -88,13 +87,11 @@
     def q_pass_near(c):
         q_copy(1, c).wait_recv()
         q_copy(3, c).start()
+
+    def q_pass_far(c):
+        q_copy(0, c).wait_recv()
+        q_copy(3, c).wait_recv()
         q_copy(4, c).start()
-        q_copy(0, c).wait_recv()
-        q_copy(5, c).start()
-
-    def q_pass_far(c):
-        q_copy(3, c).wait_recv()
-        q_copy(6, c).start()
 
     span_start = me * span
     chip_disp = (0, 4 - turn, 4 + turn, 2)
@@ -119,7 +116,7 @@
     q_own(3)
 
     def q_arrive(c):
-        for kind in (2, 4, 5, 6):
+        for kind in (2, 4):
             q_copy(kind, c).wait_recv()
 
     lane = lax.broadcasted_iota(jnp.int32, (GROUP, head_dim), 1)
@@ -169,87 +166,94 @@
                 o = o2[n * rows:(n + 1) * rows, n * head_dim:(n + 1) * head_dim] * inv[n * rows:(n + 1) * rows]
                 slab_o[pl.ds(j + n, rows, stride=PITCH), :] = o
 
-    def to_lanes(values):
+    def to_lanes(values, h, held):
         total = jnp.zeros((GROUP, head_dim), jnp.float32)
         for i, value in enumerate(values):
-            total = jnp.where(lane == seq + i * GROUP, value, total)
-        return jnp.sum(total, axis=0, keepdims=True)
-
-    def from_lanes(line, i):
-        return jnp.sum(jnp.where(lane == seq + i * GROUP, line, 0.0), axis=1, keepdims=True)
-
-    def pair_copies(c):
-        return tuple(pltpu.make_async_remote_copy(
-            src_ref=src.at[c], dst_ref=dst.at[c], send_sem=ps_sem.at[n, c], recv_sem=pr_sem.at[n, c],
-            device_id={"dup": partner}, device_id_type=MESH) for n, (src, dst) in enumerate(((pair_so, pair_ro), (pair_sl, pair_rl))))
-
-    def chip_copies(c):
-        copies = []
-        for s, (there, peer) in enumerate(((1, behind), (0, ahead), (2, across))):
-            for n, (src, dst) in enumerate(((chip_so, chip_ro), (chip_sl, chip_rl))):
-                copies.append(pltpu.make_async_remote_copy(
-                    src_ref=src.at[c, s], dst_ref=dst.at[c, there],
-                    send_sem=cs_sem.at[n, s, c], recv_sem=cr_sem.at[n, there, c],
-                    device_id={"dup": peer}, device_id_type=MESH))
-        return copies
-
-    def chip_arrivals(c):
+            total = jnp.where(lane == seq + (h * own + i) * GROUP, value, total)
+        line = jnp.sum(total, axis=0, keepdims=True)
+        line = jnp.where(lane[:1] >= h * own * GROUP, line, held[...])
+        held[...] = line
+        high = line.astype(jnp.bfloat16).astype(jnp.float32)
+        mid = (line - high).astype(jnp.bfloat16).astype(jnp.float32)
+        low = line - high - mid
+        part = seq[:8]
+        return jnp.where(part == 0, high, jnp.where(part == 1, mid, jnp.where(part == 2, low, 0.0))).astype(jnp.bfloat16)
+
+    def from_lanes(line, h, i):
+        return jnp.sum(jnp.where(lane == seq + (h * own + i) * GROUP, line, 0.0), axis=1, keepdims=True)
+
+    def joined(ref, *at):
+        return jnp.sum(ref[(*at, pl.ds(data, 8), slice(None))].astype(jnp.float32), axis=0, keepdims=True)
+
+    def pair_copy(k):
+        return pltpu.make_async_remote_copy(
+            src_ref=pair_so.at[k], dst_ref=pair_ro.at[k], send_sem=ps_sem.at[k], recv_sem=pr_sem.at[k],
+            device_id={"dup": partner}, device_id_type=MESH)
+
+    def chip_copies(k):
         return [pltpu.make_async_remote_copy(
-            src_ref=(chip_so, chip_sl)[n].at[c, s], dst_ref=(chip_ro, chip_rl)[n].at[c, s],
-            send_sem=cs_sem.at[n, s, c], recv_sem=cr_sem.at[n, s, c],
-            device_id={"dup": partner}, device_id_type=MESH) for s in range(3) for n in range(2)]
+            src_ref=chip_so.at[k, s], dst_ref=chip_ro.at[k, there], send_sem=cs_sem.at[s, k], recv_sem=cr_sem.at[there, k],
+            device_id={"dup": peer}, device_id_type=MESH) for s, there, peer in ((2, 2, across), (1, 0, ahead), (0, 1, behind))]
+
+    def chip_arrivals(k):
+        return [pltpu.make_async_remote_copy(
+            src_ref=chip_so.at[k, s], dst_ref=chip_ro.at[k, s], send_sem=cs_sem.at[s, k], recv_sem=cr_sem.at[s, k],
+            device_id={"dup": partner}, device_id_type=MESH) for s in range(3)]
 
     def slab(ref, g, row):
         return ref.at[g % RING][pl.ds(row * PITCH, GROUP), :]
 
-    spare = FINAL
-
     def place(g):
-        return (g + steps + spare) % (steps + spare)
+        at = (g + steps + SPARE) % (steps + SPARE)
+        return at // 2, at % 2
+
+    def rows_of(h, i):
+        return pl.ds(pl.multiple_of((h * own + i) * GROUP, GROUP), GROUP)
 
     def give(g):
-        c, r = place(g), g + KEEP
+        (k, h), r = place(g), g + KEEP
         for s in range(4):
             for i in range(own):
-                pair_so[c, s, i * GROUP:(i + 1) * GROUP, :] = slab(part_o, r, half + s * own + i).astype(jnp.bfloat16)
+                pair_so[k, s, rows_of(h, i), :] = slab(part_o, r, half + s * own + i).astype(jnp.bfloat16)
         for s in range(4):
-            pair_sl[c, s] = to_lanes([slab(part_l, r, half + s * own + i) for i in range(own)])
+            pair_so[k, s, pl.ds(data, 8), :] = to_lanes(
+                [slab(part_l, r, half + s * own + i) for i in range(own)], h, pair_held.at[s])
 
     def merge(g):
-        c, r = place(g), g + KEEP
+        (k, h), r = place(g), g + KEEP
         for s in (3, 1, 2, 0):
             logs = []
-            line = pair_rl[c, s]
+            line = joined(pair_ro, k, s)
             for i in range(own):
                 mine = slab(part_l, r, s * own + i)
-                theirs = from_lanes(line, i)
+                theirs = from_lanes(line, h, i)
                 top = jnp.maximum(mine, theirs)
                 w_mine, w_theirs = jnp.exp2(mine - top), jnp.exp2(theirs - top)
                 total = w_mine + w_theirs
                 o = (w_mine * slab(part_o, r, s * own + i)
-                     + w_theirs * pair_ro[c, s, i * GROUP:(i + 1) * GROUP, :].astype(jnp.float32)) / total
+                     + w_theirs * pair_ro[k, s, rows_of(h, i), :].astype(jnp.float32)) / total
                 log_total = top + jnp.log2(total)
                 if s == 0:
                     keep_o[r % KEEP, i] = o
                     keep_l[r % KEEP, i] = log_total
                 else:
-                    chip_so[c, s - 1, i * GROUP:(i + 1) * GROUP, :] = o.astype(jnp.bfloat16)
+                    chip_so[k, s - 1, rows_of(h, i), :] = o.astype(jnp.bfloat16)
                     logs.append(log_total)
             if s:
-                chip_sl[c, s - 1] = to_lanes(logs)
+                chip_so[k, s - 1, pl.ds(data, 8), :] = to_lanes(logs, h, chip_held.at[s - 1])
 
     def final(g):
-        c, r = place(g), g + KEEP
+        (k, h), r = place(g), g + KEEP
         to = pl.ds(pl.multiple_of(((g + steps) % steps) * GROUP, GROUP), GROUP)
-        lines = [chip_rl[c, s] for s in range(3)]
+        lines = [joined(chip_ro, k, s) for s in range(3)]
         for i in range(own):
-            logs = [keep_l[r % KEEP, i]] + [from_lanes(line, i) for line in lines]
+            logs = [keep_l[r % KEEP, i]] + [from_lanes(line, h, i) for line in lines]
             top = functools.reduce(jnp.maximum, logs)
             weights = [jnp.exp2(log - top) for log in logs]
             total = functools.reduce(jnp.add, weights)
             merged = weights[0] * keep_o[r % KEEP, i]
             for s in range(3):
-                merged = merged + weights[s + 1] * chip_ro[c, s, i * GROUP:(i + 1) * GROUP, :].astype(jnp.float32)
+                merged = merged + weights[s + 1] * chip_ro[k, s, rows_of(h, i), :].astype(jnp.float32)
             o_ref[i, to, :] = (merged / total).astype(jnp.bfloat16)
 
     def start_all(copies):
@@ -293,13 +297,13 @@
         key_copy(t).wait()
         value_copy(t - 2).wait()
 
-        @pl.when(t >= MERGE)
-        def _():
-            arrive_all(pair_copies(t - MERGE))
-
-        @pl.when(t >= FINAL)
-        def _():
-            arrive_all(chip_arrivals(t - FINAL))
+        @pl.when((t >= MERGE) & ((t - MERGE) % 2 == 0))
+        def _():
+            pair_copy((t - MERGE) // 2).wait_recv()
+
+        @pl.when((t >= FINAL) & ((t + FINAL) % 2 == 0))
+        def _():
+            arrive_all(chip_arrivals((t - FINAL) // 2))
 
         final(t - FINAL)
         merge(t - MERGE)
@@ -316,13 +320,13 @@
         def _():
             value_copy(t - 2 + VALUES).start()
 
-        @pl.when(t >= GIVE)
-        def _():
-            start_all(pair_copies(t - GIVE))
-
-        @pl.when(t >= MERGE)
-        def _():
-            start_all(chip_copies(t - MERGE))
+        @pl.when((t >= GIVE) & ((t - GIVE) % 2 == 1))
+        def _():
+            pair_copy((t - GIVE) // 2).start()
+
+        @pl.when((t >= MERGE) & ((t - MERGE) % 2 == 1))
+        def _():
+            start_all(chip_copies((t - MERGE) // 2))
         return carry
 
     lax.fori_loop(2, steps, step, 0)
@@ -332,41 +336,41 @@
     give(steps - GIVE)
     mix(steps - 2)
     soften(steps - 1)
-    start_all(pair_copies(steps - GIVE))
+    pair_copy(steps // 2 - 2).start()
     give(steps - 2)
     mix(steps - 1)
-    start_all(pair_copies(steps - 2))
     give(steps - 1)
-    start_all(pair_copies(steps - 1))
-
-    def last_merge(g, carry):
-        arrive_all(pair_copies(g))
-        merge(g)
-        start_all(chip_copies(g))
-        return carry
-
-    lax.fori_loop(steps - MERGE, steps, last_merge, 0)
-
-    def last_final(g, carry):
-        arrive_all(chip_arrivals(g))
-        final(g)
-        return carry
-
-    lax.fori_loop(steps - FINAL, steps, last_final, 0)
+    pair_copy(steps // 2 - 1).start()
+
+    def last_merge(k, carry):
+        pair_copy(k).wait_recv()
+        merge(2 * k)
+        merge(2 * k + 1)
+        start_all(chip_copies(k))
+        return carry
+
+    def last_final(k, carry):
+        arrive_all(chip_arrivals(k))
+        final(2 * k)
+        final(2 * k + 1)
+        return carry
+
+    lax.fori_loop((steps - MERGE) // 2, steps // 2, last_merge, 0)
+    lax.fori_loop((steps - FINAL) // 2, steps // 2, last_final, 0)
 
     def drain_asks(c, carry):
-        for kind in range(7):
+        for kind in range(5):
             q_copy(kind, c).wait_send()
         return carry
 
     lax.fori_loop(0, asks, drain_asks, 0)
 
-    def drain(c, carry):
-        for copy in pair_copies(c) + tuple(chip_copies(c)):
+    def drain(k, carry):
+        for copy in [pair_copy(k)] + chip_copies(k):
             copy.wait_send()
         return carry
 
-    lax.fori_loop(0, steps, drain, 0)
+    lax.fori_loop(0, steps // 2, drain, 0)
 
 
 def solution(mesh):
@@ -375,7 +379,8 @@
         span = k_span.shape[1]
         steps = num_batch // GROUP
         asks = steps // ASK
-        places = steps + FINAL
+        places = (steps + SPARE) // 2
+        block = 2 * own * GROUP + 8
         rows = 8 * own
         vmem = functools.partial(pl.BlockSpec, memory_space=pltpu.VMEM)
         hbm = functools.partial(pl.BlockSpec, memory_space=pl.ANY)
@@ -397,20 +402,18 @@
                 pltpu.VMEM((GROUP // 2, 2 * rows, head_dim), f32),
                 pltpu.VMEM((RING, rows * PITCH, head_dim), f32),
                 pltpu.VMEM((RING, rows * PITCH, head_dim), f32),
-                pltpu.VMEM((places, 4, own * GROUP, head_dim), bf16),
-                pltpu.VMEM((places, 4, 1, head_dim), f32),
-                pltpu.VMEM((places, 4, own * GROUP, head_dim), bf16),
-                pltpu.VMEM((places, 4, 1, head_dim), f32),
-                pltpu.VMEM((places, 3, own * GROUP, head_dim), bf16),
-                pltpu.VMEM((places, 3, 1, head_dim), f32),
-                pltpu.VMEM((places, 3, own * GROUP, head_dim), bf16),
-                pltpu.VMEM((places, 3, 1, head_dim), f32),
+                pltpu.VMEM((places, 4, block, head_dim), bf16),
+                pltpu.VMEM((places, 4, block, head_dim), bf16),
+                pltpu.VMEM((places, 3, block, head_dim), bf16),
+                pltpu.VMEM((places, 3, block, head_dim), bf16),
+                pltpu.VMEM((4, 1, head_dim), f32),
+                pltpu.VMEM((3, 1, head_dim), f32),
                 pltpu.VMEM((KEEP, own, GROUP, head_dim), f32),
                 pltpu.VMEM((KEEP, own, GROUP, head_dim), f32),
                 dma((KEYS,)), dma((VALUES,)),
-                dma((7, asks)), dma((7, asks)),
-                dma((2, steps)), dma((2, steps)),
-                dma((2, 3, steps)), dma((2, 3, steps)),
+                dma((5, asks)), dma((5, asks)),
+                dma((steps // 2,)), dma((steps // 2,)),
+                dma((3, steps // 2)), dma((3, steps // 2)),
             ],
             compiler_params=pltpu.CompilerParams(
                 collective_id=0, has_side_effects=True, vmem_limit_bytes=60 * 1024 * 1024),

time: 50.5 us -> 48.1 us (0.952)
  Pallas kernels: 48.8 us -> 46.4 us
    pallas_call x1, Pallas kernels: 48.8 us -> 46.4 us  [group_step(): pl.pallas_call(attend, out_shape=jax.ShapeDtypeStruct((own, num_batch, he...]
where the time goes in v6:
time: 48.1 us; the launch traced here: 48 us
  Pallas kernels  46.4 us (96%)
  local copies, waits for them, and re-layouts  1.62 us (3%)
    pallas_call x1, Pallas kernels, group_step(): pl.pallas_call(attend, out_shape=jax.ShapeDtypeStruct((own, num_batch, he...  46.4 us
    unnamed x1, local copies, waits for them, and re-layouts  1.62 us

profile of v6, /device:TPU:112, one launch (start us, length us, event | category | flops | bytes accessed | tf_op | source)
XLA Modules:
  0.0 48.0 jit_solution(17655031013631414087)
XLA Ops:
  0.0 46.4 %shard_map.46 = bf16[3,256,128]{2,1,0:T(8,128)(2,1)} custom-call(bf16[3,256,128]{2,1,0:T(8,128)(2,1)} %bitcast.3, s32[256]{0:T(256)} %len_ref.1, bf16[256,512,128]{2,1,0:T(8,128)(2,1)} %k_hbm.1, bf16[256,512,128]{2,1,0:T(8,128)(2,1)} %v_hbm.1), custom_call_target="tpu_custom_call" | custom-call | flops 1610612736 | bytes 67108864 | tf_op jit(solution)/shard_map/pallas_call | solution.py:389
  46.4 1.6 %copy.6 = bf16[256,3,128]{2,0,1:T(8,128)(2,1)} copy(bf16[256,3,128]{2,0,1:T(8,128)(2,1)} %bitcast.2) | data formatting | bytes 393216

commit v7 on v6

v7 whole, which is shorter than its diff:
```python
import functools

import jax
import jax.numpy as jnp
from jax import lax
from jax.experimental import pallas as pl
from jax.experimental.pallas import tpu as pltpu
from jax.sharding import PartitionSpec as P

DRAFT = 4
NEG_BIG = -3e38
LOG2E = 1.4426950408889634
MESH = pl.DeviceIdType.MESH

GROUP = 16
KEYS = 10
VALUES = 11
PITCH = GROUP + 4
RING = 8
KEEP = 16
ASK = 2
GIVE, MERGE, HALVE, FINAL = 2, 4, 7, 10
SPARE = 10


def attend(q_ref, len_ref, k_hbm, v_hbm, o_ref,
           kbuf, vbuf, q_all, q_wide, pos_rel, s_buf, p_buf, i_buf, part_o, part_l,
           pair_so, pair_ro, near_so, near_ro, far_so, far_ro, keep_o, keep_l, last_o, last_l,
           k_sem, v_sem, qs_sem, qr_sem, pair_sem, near_sem, far_sem):
    own, num_batch, head_dim = q_ref.shape
    span = k_hbm.shape[1]
    rows = 8 * own
    half = 4 * own
    data = own * GROUP
    steps = num_batch // GROUP
    asks = steps // ASK
    scale = (head_dim ** -0.5) * LOG2E

    me = lax.axis_index("dup")
    chip = me // 2
    core = me % 2
    turn = (1 - 2 * core) * (1 - 2 * (chip % 2))
    partner = chip * 2 + (1 - core)
    ahead = ((chip + turn + 4) % 4) * 2 + core
    behind = ((chip - turn + 4) % 4) * 2 + core

    def key_copy(g):
        return pltpu.make_async_copy(k_hbm.at[pl.ds(g * GROUP, GROUP)], kbuf.at[g % KEYS], k_sem.at[g % KEYS])

    def value_copy(g):
        return pltpu.make_async_copy(v_hbm.at[pl.ds(g * GROUP, GROUP)], vbuf.at[g % VALUES], v_sem.at[g % VALUES])

    key_copy(0).start()
    key_copy(1).start()

    def start_cache(g, carry):
        key_copy(g + 2).start()
        value_copy(g).start()
        return carry

    lax.fori_loop(0, KEYS - 2, start_cache, 0)
    for g in range(KEYS - 2, VALUES):
        value_copy(g).start()

    barrier = pltpu.get_barrier_semaphore()
    for peer in (partner, ahead, behind):
        pl.semaphore_signal(barrier, inc=1, device_id={"dup": peer}, device_id_type=MESH)

    def q_copy(kind, c):
        part = pl.ds(pl.multiple_of(c * ASK * GROUP, ASK * GROUP), ASK * GROUP)
        src, dst, peer = (
            (q_ref.at[:, part], q_all.at[1, :, part], behind),
            (q_ref.at[:, part], q_all.at[2, :, part], ahead),
            (q_ref.at[:, part], q_all.at[4, :, part], partner),
            (q_all.at[1, :, part], q_all.at[3, :, part], ahead),
            (q_all.at[1:4, :, part], q_all.at[5:8, :, part], partner),
        )[kind]
        return pltpu.make_async_remote_copy(
            src_ref=src, dst_ref=dst, send_sem=qs_sem.at[kind, c], recv_sem=qr_sem.at[kind, c],
            device_id={"dup": peer}, device_id_type=MESH)

    def q_own(c):
        for kind in (0, 1, 2):
            q_copy(kind, c).start()

    def q_pass_near(c):
        q_copy(0, c).wait_recv()
        q_copy(3, c).start()

    def q_pass_far(c):
        q_copy(1, c).wait_recv()
        q_copy(3, c).wait_recv()
        q_copy(4, c).start()

    span_start = me * span
    chip_disp = (0, 4 - turn, 4 + turn, 2)
    pair_disp = (0, 4 + turn, 4 - turn, 2)
    row_id = lax.broadcasted_iota(jnp.int32, (rows, span), 0)
    token = jnp.zeros((rows, span), jnp.int32)
    for h in range(2):
        for s in range(4):
            disp = (chip_disp, pair_disp)[h][s]
            device = ((chip + disp) % 4) * 2 + (core if h == 0 else 1 - core)
            for i in range(own):
                token = jnp.where(row_id == h * half + s * own + i, (own * device + i) % DRAFT, token)
    pos_rel[...] = lax.broadcasted_iota(jnp.int32, (rows, span), 1) + span_start - token

    pl.semaphore_wait(barrier, 3)
    q_own(0)
    q_own(1)
    q_pass_near(0)
    q_pass_far(0)
    q_pass_near(1)
    q_own(2)
    q_own(3)

    def q_arrive(c):
        for kind in (2, 4):
            q_copy(kind, c).wait_recv()

    lane = lax.broadcasted_iota(jnp.int32, (GROUP, head_dim), 1)
    seq = lax.broadcasted_iota(jnp.int32, (GROUP, head_dim), 0)

    def score(g):
        part = pl.ds(pl.multiple_of(g * GROUP, GROUP), GROUP)
        for s in range(8):
            for i in range(own):
                block = q_ref[i, part, :] if s == 0 else q_all[s, i, part, :]
                q_wide[pl.ds((s * own + i) * PITCH, GROUP), :] = block.astype(jnp.float32)
        slot = g % KEYS
        zeros = jnp.zeros((rows, head_dim), jnp.float32)
        for j in range(0, GROUP, 2):
            q0 = q_wide[pl.ds(j, rows, stride=PITCH), :]
            q1 = q_wide[pl.ds(j + 1, rows, stride=PITCH), :]
            q2 = jnp.concatenate([jnp.concatenate([q0, zeros], 1), jnp.concatenate([zeros, q1], 1)], 0).astype(jnp.bfloat16)
            k2 = jnp.concatenate([kbuf[slot, j], kbuf[slot, j + 1]], 1)
            s_buf[j // 2] = lax.dot_general(q2, k2, (((1,), (1,)), ((), ())), preferred_element_type=jnp.float32)

    def soften(g):
        slab_l = part_l.at[g % RING]
        for j in range(0, GROUP, 2):
            s = s_buf[j // 2]
            rel = pos_rel[...]
            base = g * GROUP + j
            s = jnp.concatenate([
                jnp.where(rel <= len_ref[base] - DRAFT, s[:rows], NEG_BIG),
                jnp.where(rel <= len_ref[base + 1] - DRAFT, s[rows:], NEG_BIG)], 0)
            peak = jnp.max(s, axis=1, keepdims=True)
            p = jnp.exp2((s - peak) * scale)
            mass = jnp.sum(p, axis=1, keepdims=True)
            p_buf[j // 2] = p.astype(jnp.bfloat16)
            i_buf[j // 2] = jnp.broadcast_to(1.0 / mass, (2 * rows, head_dim))
            log_mass = jnp.broadcast_to(peak * scale + jnp.log2(mass), (2 * rows, head_dim))
            for n in range(2):
                slab_l[pl.ds(j + n, rows, stride=PITCH), :] = log_mass[n * rows:(n + 1) * rows]

    def mix(g):
        slot = g % VALUES
        slab_o = part_o.at[g % RING]
        for j in range(0, GROUP, 2):
            v2 = jnp.concatenate([vbuf[slot, j], vbuf[slot, j + 1]], 1)
            o2 = jnp.dot(p_buf[j // 2], v2, preferred_element_type=jnp.float32)
            inv = i_buf[j // 2]
            for n in range(2):
                o = o2[n * rows:(n + 1) * rows, n * head_dim:(n + 1) * head_dim] * inv[n * rows:(n + 1) * rows]
                slab_o[pl.ds(j + n, rows, stride=PITCH), :] = o

    def to_lanes(values):
        total = jnp.zeros((GROUP, head_dim), jnp.float32)
        for i, value in enumerate(values):
            total = jnp.where(lane == seq + i * GROUP, value, total)
        line = jnp.sum(total, axis=0, keepdims=True)
        high = line.astype(jnp.bfloat16).astype(jnp.float32)
        mid = (line - high).astype(jnp.bfloat16).astype(jnp.float32)
        low = line - high - mid
        part = seq[:8]
        return jnp.where(part == 0, high, jnp.where(part == 1, mid, jnp.where(part == 2, low, 0.0))).astype(jnp.bfloat16)

    def put(ref, values, logs):
        for i, value in enumerate(values):
            ref[i * GROUP:(i + 1) * GROUP, :] = value.astype(jnp.bfloat16)
        ref[data:data + 8, :] = to_lanes(logs)

    def take(ref):
        line = jnp.sum(ref[data:data + 8, :].astype(jnp.float32), axis=0, keepdims=True)
        return [(ref[i * GROUP:(i + 1) * GROUP, :].astype(jnp.float32),
                 jnp.sum(jnp.where(lane == seq + i * GROUP, line, 0.0), axis=1, keepdims=True)) for i in range(own)]

    def joined(mine, log_mine, theirs, log_theirs):
        top = jnp.maximum(log_mine, log_theirs)
        w_mine, w_theirs = jnp.exp2(log_mine - top), jnp.exp2(log_theirs - top)
        total = w_mine + w_theirs
        return (w_mine * mine + w_theirs * theirs) / total, top + jnp.log2(total)

    def copy_of(src, dst, sems, c, peer):
        return pltpu.make_async_remote_copy(
            src_ref=src.at[c], dst_ref=dst.at[c], send_sem=sems.at[0, c], recv_sem=sems.at[1, c],
            device_id={"dup": peer}, device_id_type=MESH)

    def pair_copy(c):
        return copy_of(pair_so, pair_ro, pair_sem, c, partner)

    def near_copy(c):
        return copy_of(near_so, near_ro, near_sem, c, behind)

    def far_copy(c):
        return copy_of(far_so, far_ro, far_sem, c, ahead)

    def slab(ref, g, row):
        return ref.at[g % RING][pl.ds(row * PITCH, GROUP), :]

    def place(g):
        return (g + steps + SPARE) % (steps + SPARE)

    def give(g):
        c, r = place(g), g + KEEP
        for s in range(4):
            at = [half + s * own + i for i in range(own)]
            put(pair_so.at[c, s], [slab(part_o, r, n) for n in at], [slab(part_l, r, n) for n in at])

    def merge(g):
        c, r = place(g), g + KEEP
        for s in (1, 3, 0, 2):
            both = [joined(slab(part_o, r, s * own + i), slab(part_l, r, s * own + i), *theirs)
                    for i, theirs in enumerate(take(pair_ro.at[c, s]))]
            if s % 2:
                put(near_so.at[c, s // 2], [o for o, _ in both], [log for _, log in both])
            else:
                for i, (o, log) in enumerate(both):
                    keep_o[r % KEEP, s // 2, i] = o
                    keep_l[r % KEEP, s // 2, i] = log

    def halve(g):
        c, r = place(g), g + KEEP
        for s in (1, 0):
            both = [joined(keep_o[r % KEEP, s, i], keep_l[r % KEEP, s, i], *theirs)
                    for i, theirs in enumerate(take(near_ro.at[c, s]))]
            if s:
                put(far_so.at[c], [o for o, _ in both], [log for _, log in both])
            else:
                for i, (o, log) in enumerate(both):
                    last_o[r % KEEP, i] = o
                    last_l[r % KEEP, i] = log

    def final(g):
        c, r = place(g), g + KEEP
        to = pl.ds(pl.multiple_of(((g + steps) % steps) * GROUP, GROUP), GROUP)
        for i, theirs in enumerate(take(far_ro.at[c])):
            o_ref[i, to, :] = joined(last_o[r % KEEP, i], last_l[r % KEEP, i], *theirs)[0].astype(jnp.bfloat16)

    q_arrive(0)
    key_copy(0).wait()
    score(0)
    key_copy(KEYS).start()
    key_copy(1).wait()
    soften(0)
    score(1)
    key_copy(KEYS + 1).start()
    q_pass_far(1)
    q_pass_near(2)

    def step(t, carry):
        c = t // ASK

        @pl.when(t % ASK == 0)
        def _():
            @pl.when(c + 3 < asks)
            def _():
                q_own(c + 3)

            @pl.when(c + 2 < asks)
            def _():
                q_pass_near(c + 2)

            @pl.when(c + 1 < asks)
            def _():
                q_pass_far(c + 1)

            q_arrive(c)

        key_copy(t).wait()
        value_copy(t - 2).wait()

        @pl.when(t >= MERGE)
        def _():
            pair_copy(t - MERGE).wait_recv()

        @pl.when(t >= HALVE)
        def _():
            near_copy(t - HALVE).wait_recv()

        @pl.when(t >= FINAL)
        def _():
            far_copy(t - FINAL).wait_recv()

        final(t - FINAL)
        halve(t - HALVE)
        merge(t - MERGE)
        mix(t - 2)
        give(t - GIVE)
        soften(t - 1)
        score(t)

        pair_copy(t - GIVE).start()

        @pl.when(t >= MERGE)
        def _():
            near_copy(t - MERGE).start()

        @pl.when(t >= HALVE)
        def _():
            far_copy(t - HALVE).start()

        @pl.when(t + KEYS < steps)
        def _():
            key_copy(t + KEYS).start()

        @pl.when(t - 2 + VALUES < steps)
        def _():
            value_copy(t - 2 + VALUES).start()
        return carry

    lax.fori_loop(2, steps, step, 0)

    def late_merge(g):
        pair_copy(g).wait_recv()
        merge(g)
        near_copy(g).start()

    def late_halve(g):
        near_copy(g).wait_recv()
        halve(g)
        far_copy(g).start()

    def late_final(g, carry):
        far_copy(g).wait_recv()
        final(g)
        return carry

    value_copy(steps - 2).wait()
    mix(steps - 2)
    give(steps - 2)
    soften(steps - 1)
    pair_copy(steps - 2).start()
    value_copy(steps - 1).wait()
    mix(steps - 1)
    give(steps - 1)
    pair_copy(steps - 1).start()

    def late_step(j, carry):
        late_merge(steps - MERGE + j)
        late_halve(steps - HALVE + j)
        return carry

    lax.fori_loop(0, MERGE, late_step, 0)
    lax.fori_loop(steps - FINAL, steps - HALVE, late_final, 0)

    def later_step(j, carry):
        late_halve(steps - 3 + j)
        return late_final(steps - HALVE + j, carry)

    lax.fori_loop(0, 3, later_step, 0)
    lax.fori_loop(steps - HALVE + 3, steps, late_final, 0)

    def drain_asks(c, carry):
        for kind in range(5):
            q_copy(kind, c).wait_send()
        return carry

    lax.fori_loop(0, asks, drain_asks, 0)

    def drain(c, carry):
        for copy in (pair_copy(c), near_copy(c), far_copy(c)):
            copy.wait_send()
        return carry

    lax.fori_loop(0, steps, drain, 0)


def solution(mesh):
    def group_step(q_local, k_span, v_span, len_local):
        num_batch, own, head_dim = q_local.shape
        span = k_span.shape[1]
        steps = num_batch // GROUP
        asks = steps // ASK
        places = steps + SPARE
        block = own * GROUP + 8
        rows = 8 * own
        vmem = functools.partial(pl.BlockSpec, memory_space=pltpu.VMEM)
        hbm = functools.partial(pl.BlockSpec, memory_space=pl.ANY)
        bf16, f32 = jnp.bfloat16, jnp.float32
        dma = pltpu.SemaphoreType.DMA
        out = pl.pallas_call(
            attend,
            out_shape=jax.ShapeDtypeStruct((own, num_batch, head_dim), bf16),
            in_specs=[vmem(), pl.BlockSpec(memory_space=pltpu.SMEM), hbm(), hbm()],
            out_specs=vmem(),
            scratch_shapes=[
                pltpu.VMEM((KEYS, GROUP, span, head_dim), bf16),
                pltpu.VMEM((VALUES, GROUP, span, head_dim), bf16),
                pltpu.VMEM((8, own, num_batch, head_dim), bf16),
                pltpu.VMEM((rows * PITCH, head_dim), f32),
                pltpu.VMEM((rows, span), jnp.int32),
                pltpu.VMEM((GROUP // 2, 2 * rows, span), f32),
                pltpu.VMEM((GROUP // 2, 2 * rows, span), bf16),
                pltpu.VMEM((GROUP // 2, 2 * rows, head_dim), f32),
                pltpu.VMEM((RING, rows * PITCH, head_dim), f32),
                pltpu.VMEM((RING, rows * PITCH, head_dim), f32),
                pltpu.VMEM((places, 4, block, head_dim), bf16),
                pltpu.VMEM((places, 4, block, head_dim), bf16),
                pltpu.VMEM((places, 2, block, head_dim), bf16),
                pltpu.VMEM((places, 2, block, head_dim), bf16),
                pltpu.VMEM((places, block, head_dim), bf16),
                pltpu.VMEM((places, block, head_dim), bf16),
                pltpu.VMEM((KEEP, 2, own, GROUP, head_dim), f32),
                pltpu.VMEM((KEEP, 2, own, GROUP, head_dim), f32),
                pltpu.VMEM((KEEP, own, GROUP, head_dim), f32),
                pltpu.VMEM((KEEP, own, GROUP, head_dim), f32),
                dma((KEYS,)), dma((VALUES,)),
                dma((5, asks)), dma((5, asks)),
                dma((2, steps)), dma((2, steps)), dma((2, steps)),
            ],
            compiler_params=pltpu.CompilerParams(
                collective_id=0, has_side_effects=True, vmem_limit_bytes=60 * 1024 * 1024),
            cost_estimate=pl.CostEstimate(
                flops=4 * num_batch * rows * span * head_dim,
                bytes_accessed=4 * num_batch * span * head_dim,
                transcendentals=num_batch * rows * span),
        )(q_local.transpose(1, 0, 2), len_local, k_span, v_span)
        return out.transpose(1, 0, 2)

    return jax.shard_map(
        group_step, mesh=mesh,
        in_specs=(P("kv", "dup", None), P("kv", "dup", None), P("kv", "dup", None), P("kv")),
        out_specs=P("kv", "dup", None), check_vma=False)
```

time: 48.1 us -> 51.3 us (1.067)
  Pallas kernels: 46.4 us -> 49.3 us
    pallas_call x1, Pallas kernels: 46.4 us -> 49.3 us  [group_step(): pl.pallas_call(attend, out_shape=jax.ShapeDtypeStruct((own, num_batch, he...]
where the time goes in v7:
time: 51.3 us; the launch traced here: 50.9 us
  Pallas kernels  49.3 us (96%)
  local copies, waits for them, and re-layouts  1.62 us (3%)
    pallas_call x1, Pallas kernels, group_step(): pl.pallas_call(attend, out_shape=jax.ShapeDtypeStruct((own, num_batch, he...  49.3 us
    unnamed x1, local copies, waits for them, and re-layouts  1.62 us

profile of v7, /device:TPU:112, one launch (start us, length us, event | category | flops | bytes accessed | tf_op | source)
XLA Modules:
  0.0 50.9 jit_solution(6592084443345743421)
XLA Ops:
  0.0 49.3 %shard_map.46 = bf16[3,256,128]{2,1,0:T(8,128)(2,1)} custom-call(bf16[3,256,128]{2,1,0:T(8,128)(2,1)} %bitcast.3, s32[256]{0:T(256)} %len_ref.1, bf16[256,512,128]{2,1,0:T(8,128)(2,1)} %k_hbm.1, bf16[256,512,128]{2,1,0:T(8,128)(2,1)} %v_hbm.1), custom_call_target="tpu_custom_call" | custom-call | flops 1610612736 | bytes 67108864 | tf_op jit(solution)/shard_map/pallas_call | solution.py:393
  49.3 1.6 %copy.6 = bf16[256,3,128]{2,0,1:T(8,128)(2,1)} copy(bf16[256,3,128]{2,0,1:T(8,128)(2,1)} %bitcast.2) | data formatting | bytes 393216

commit v8 on v7

--- a/solution.py
+++ b/solution.py
@@ -19,14 +19,14 @@
 RING = 8
 KEEP = 16
 ASK = 2
-GIVE, MERGE, HALVE, FINAL = 2, 4, 7, 10
-SPARE = 10
+GIVE, MERGE, FINAL = 2, 4, 9
+SPARE = 9
 
 
 def attend(q_ref, len_ref, k_hbm, v_hbm, o_ref,
            kbuf, vbuf, q_all, q_wide, pos_rel, s_buf, p_buf, i_buf, part_o, part_l,
-           pair_so, pair_ro, near_so, near_ro, far_so, far_ro, keep_o, keep_l, last_o, last_l,
-           k_sem, v_sem, qs_sem, qr_sem, pair_sem, near_sem, far_sem):
+           pair_so, pair_ro, chip_so, chip_ro, keep_o, keep_l,
+           k_sem, v_sem, qs_sem, qr_sem, pair_sem, chip_sem):
     own, num_batch, head_dim = q_ref.shape
     span = k_hbm.shape[1]
     rows = 8 * own
@@ -43,6 +43,7 @@
     partner = chip * 2 + (1 - core)
     ahead = ((chip + turn + 4) % 4) * 2 + core
     behind = ((chip - turn + 4) % 4) * 2 + core
+    across = ((chip + 2) % 4) * 2 + core
 
     def key_copy(g):
         return pltpu.make_async_copy(k_hbm.at[pl.ds(g * GROUP, GROUP)], kbuf.at[g % KEYS], k_sem.at[g % KEYS])
@@ -63,10 +64,10 @@
         value_copy(g).start()
 
     barrier = pltpu.get_barrier_semaphore()
-    for peer in (partner, ahead, behind):
+    for peer in (partner, ahead, behind, across):
         pl.semaphore_signal(barrier, inc=1, device_id={"dup": peer}, device_id_type=MESH)
 
-    def q_copy(kind, c):
+    def q_copy(kind, c, direct=False):
         part = pl.ds(pl.multiple_of(c * ASK * GROUP, ASK * GROUP), ASK * GROUP)
         src, dst, peer = (
             (q_ref.at[:, part], q_all.at[1, :, part], behind),
@@ -75,6 +76,8 @@
             (q_all.at[1, :, part], q_all.at[3, :, part], ahead),
             (q_all.at[1:4, :, part], q_all.at[5:8, :, part], partner),
         )[kind]
+        if direct:
+            src, peer = q_ref.at[:, part], across
         return pltpu.make_async_remote_copy(
             src_ref=src, dst_ref=dst, send_sem=qs_sem.at[kind, c], recv_sem=qr_sem.at[kind, c],
             device_id={"dup": peer}, device_id_type=MESH)
@@ -105,14 +108,15 @@
                 token = jnp.where(row_id == h * half + s * own + i, (own * device + i) % DRAFT, token)
     pos_rel[...] = lax.broadcasted_iota(jnp.int32, (rows, span), 1) + span_start - token
 
-    pl.semaphore_wait(barrier, 3)
+    pl.semaphore_wait(barrier, 4)
+    q_copy(3, 0, direct=True).start()
     q_own(0)
-    q_own(1)
-    q_pass_near(0)
+    for c in range(1, 6):
+        q_own(c)
+    q_copy(0, 0).wait_recv()
     q_pass_far(0)
     q_pass_near(1)
-    q_own(2)
-    q_own(3)
+    q_pass_near(2)
 
     def q_arrive(c):
         for kind in (2, 4):
@@ -200,11 +204,18 @@
     def pair_copy(c):
         return copy_of(pair_so, pair_ro, pair_sem, c, partner)
 
-    def near_copy(c):
-        return copy_of(near_so, near_ro, near_sem, c, behind)
-
-    def far_copy(c):
-        return copy_of(far_so, far_ro, far_sem, c, ahead)
+    def chip_copies(c):
+        return [pltpu.make_async_remote_copy(
+            src_ref=chip_so.at[c, n], dst_ref=chip_ro.at[c, n], send_sem=chip_sem.at[0, n, c], recv_sem=chip_sem.at[1, n, c],
+            device_id={"dup": peer}, device_id_type=MESH) for n, peer in ((2, across), (0, behind), (1, ahead))]
+
+    def chip_start(c):
+        for copy in chip_copies(c):
+            copy.start()
+
+    def chip_arrive(c):
+        for copy in chip_copies(c):
+            copy.wait_recv()
 
     def slab(ref, g, row):
         return ref.at[g % RING][pl.ds(row * PITCH, GROUP), :]
@@ -220,33 +231,29 @@
 
     def merge(g):
         c, r = place(g), g + KEEP
-        for s in (1, 3, 0, 2):
+        for s in (3, 1, 2, 0):
             both = [joined(slab(part_o, r, s * own + i), slab(part_l, r, s * own + i), *theirs)
                     for i, theirs in enumerate(take(pair_ro.at[c, s]))]
-            if s % 2:
-                put(near_so.at[c, s // 2], [o for o, _ in both], [log for _, log in both])
+            if s:
+                put(chip_so.at[c, s - 1], [o for o, _ in both], [log for _, log in both])
             else:
                 for i, (o, log) in enumerate(both):
-                    keep_o[r % KEEP, s // 2, i] = o
-                    keep_l[r % KEEP, s // 2, i] = log
-
-    def halve(g):
-        c, r = place(g), g + KEEP
-        for s in (1, 0):
-            both = [joined(keep_o[r % KEEP, s, i], keep_l[r % KEEP, s, i], *theirs)
-                    for i, theirs in enumerate(take(near_ro.at[c, s]))]
-            if s:
-                put(far_so.at[c], [o for o, _ in both], [log for _, log in both])
-            else:
-                for i, (o, log) in enumerate(both):
-                    last_o[r % KEEP, i] = o
-                    last_l[r % KEEP, i] = log
+                    keep_o[r % KEEP, i] = o
+                    keep_l[r % KEEP, i] = log
 
     def final(g):
         c, r = place(g), g + KEEP
         to = pl.ds(pl.multiple_of(((g + steps) % steps) * GROUP, GROUP), GROUP)
-        for i, theirs in enumerate(take(far_ro.at[c])):
-            o_ref[i, to, :] = joined(last_o[r % KEEP, i], last_l[r % KEEP, i], *theirs)[0].astype(jnp.bfloat16)
+        others = [take(chip_ro.at[c, n]) for n in range(3)]
+        for i in range(own):
+            logs = [keep_l[r % KEEP, i]] + [other[i][1] for other in others]
+            top = functools.reduce(jnp.maximum, logs)
+            weights = [jnp.exp2(log - top) for log in logs]
+            total = functools.reduce(jnp.add, weights)
+            merged = weights[0] * keep_o[r % KEEP, i]
+            for weight, other in zip(weights[1:], others):
+                merged = merged + weight * other[i][0]
+            o_ref[i, to, :] = (merged / total).astype(jnp.bfloat16)
 
     q_arrive(0)
     key_copy(0).wait()
@@ -257,20 +264,20 @@
     score(1)
     key_copy(KEYS + 1).start()
     q_pass_far(1)
-    q_pass_near(2)
+    q_pass_near(3)
 
     def step(t, carry):
         c = t // ASK
 
         @pl.when(t % ASK == 0)
         def _():
+            @pl.when(c + 5 < asks)
+            def _():
+                q_own(c + 5)
+
             @pl.when(c + 3 < asks)
             def _():
-                q_own(c + 3)
-
-            @pl.when(c + 2 < asks)
-            def _():
-                q_pass_near(c + 2)
+                q_pass_near(c + 3)
 
             @pl.when(c + 1 < asks)
             def _():
@@ -285,16 +292,11 @@
         def _():
             pair_copy(t - MERGE).wait_recv()
 
-        @pl.when(t >= HALVE)
-        def _():
-            near_copy(t - HALVE).wait_recv()
-
         @pl.when(t >= FINAL)
         def _():
-            far_copy(t - FINAL).wait_recv()
+            chip_arrive(t - FINAL)
 
         final(t - FINAL)
-        halve(t - HALVE)
         merge(t - MERGE)
         mix(t - 2)
         give(t - GIVE)
@@ -305,11 +307,7 @@
 
         @pl.when(t >= MERGE)
         def _():
-            near_copy(t - MERGE).start()
-
-        @pl.when(t >= HALVE)
-        def _():
-            far_copy(t - HALVE).start()
+            chip_start(t - MERGE)
 
         @pl.when(t + KEYS < steps)
         def _():
@@ -322,18 +320,14 @@
 
     lax.fori_loop(2, steps, step, 0)
 
-    def late_merge(g):
+    def late_merge(g, carry):
         pair_copy(g).wait_recv()
         merge(g)
-        near_copy(g).start()
-
-    def late_halve(g):
-        near_copy(g).wait_recv()
-        halve(g)
-        far_copy(g).start()
+        chip_start(g)
+        return carry
 
     def late_final(g, carry):
-        far_copy(g).wait_recv()
+        chip_arrive(g)
         final(g)
         return carry
 
@@ -347,20 +341,8 @@
     give(steps - 1)
     pair_copy(steps - 1).start()
 
-    def late_step(j, carry):
-        late_merge(steps - MERGE + j)
-        late_halve(steps - HALVE + j)
-        return carry
-
-    lax.fori_loop(0, MERGE, late_step, 0)
-    lax.fori_loop(steps - FINAL, steps - HALVE, late_final, 0)
-
-    def later_step(j, carry):
-        late_halve(steps - 3 + j)
-        return late_final(steps - HALVE + j, carry)
-
-    lax.fori_loop(0, 3, later_step, 0)
-    lax.fori_loop(steps - HALVE + 3, steps, late_final, 0)
+    lax.fori_loop(steps - MERGE, steps, late_merge, 0)
+    lax.fori_loop(steps - FINAL, steps, late_final, 0)
 
     def drain_asks(c, carry):
         for kind in range(5):
@@ -370,7 +352,7 @@
     lax.fori_loop(0, asks, drain_asks, 0)
 
     def drain(c, carry):
-        for copy in (pair_copy(c), near_copy(c), far_copy(c)):
+        for copy in [pair_copy(c)] + chip_copies(c):
             copy.wait_send()
         return carry
 
@@ -408,17 +390,13 @@
                 pltpu.VMEM((RING, rows * PITCH, head_dim), f32),
                 pltpu.VMEM((places, 4, block, head_dim), bf16),
                 pltpu.VMEM((places, 4, block, head_dim), bf16),
-                pltpu.VMEM((places, 2, block, head_dim), bf16),
-                pltpu.VMEM((places, 2, block, head_dim), bf16),
-                pltpu.VMEM((places, block, head_dim), bf16),
-                pltpu.VMEM((places, block, head_dim), bf16),
-                pltpu.VMEM((KEEP, 2, own, GROUP, head_dim), f32),
-                pltpu.VMEM((KEEP, 2, own, GROUP, head_dim), f32),
+                pltpu.VMEM((places, 3, block, head_dim), bf16),
+                pltpu.VMEM((places, 3, block, head_dim), bf16),
                 pltpu.VMEM((KEEP, own, GROUP, head_dim), f32),
                 pltpu.VMEM((KEEP, own, GROUP, head_dim), f32),
                 dma((KEYS,)), dma((VALUES,)),
                 dma((5, asks)), dma((5, asks)),
-                dma((2, steps)), dma((2, steps)), dma((2, steps)),
+                dma((2, steps)), dma((2, 3, steps)),
             ],
             compiler_params=pltpu.CompilerParams(
                 collective_id=0, has_side_effects=True, vmem_limit_bytes=60 * 1024 * 1024),

time: 51.3 us -> 42.3 us (0.82)
  Pallas kernels: 49.3 us -> 40.5 us
    pallas_call x1, Pallas kernels: 49.3 us -> 40.5 us  [group_step(): pl.pallas_call(attend, out_shape=jax.ShapeDtypeStruct((own, num_batch, he...]
where the time goes in v8:
time: 42.3 us; the launch traced here: 42.1 us
  Pallas kernels  40.5 us (96%)
  local copies, waits for them, and re-layouts  1.62 us (4%)
    pallas_call x1, Pallas kernels, group_step(): pl.pallas_call(attend, out_shape=jax.ShapeDtypeStruct((own, num_batch, he...  40.5 us
    unnamed x1, local copies, waits for them, and re-layouts  1.62 us

profile of v8, /device:TPU:112, one launch (start us, length us, event | category | flops | bytes accessed | tf_op | source)
XLA Modules:
  0.0 42.1 jit_solution(8972382749769796349)
XLA Ops:
  0.0 40.5 %shard_map.46 = bf16[3,256,128]{2,1,0:T(8,128)(2,1)} custom-call(bf16[3,256,128]{2,1,0:T(8,128)(2,1)} %bitcast.3, s32[256]{0:T(256)} %len_ref.1, bf16[256,512,128]{2,1,0:T(8,128)(2,1)} %k_hbm.1, bf16[256,512,128]{2,1,0:T(8,128)(2,1)} %v_hbm.1), custom_call_target="tpu_custom_call" | custom-call | flops 1610612736 | bytes 67108864 | tf_op jit(solution)/shard_map/pallas_call | solution.py:375
  40.5 1.6 %copy.6 = bf16[256,3,128]{2,0,1:T(8,128)(2,1)} copy(bf16[256,3,128]{2,0,1:T(8,128)(2,1)} %bitcast.2) | data formatting | bytes 393216

commit v9 on v8

--- a/solution.py
+++ b/solution.py
@@ -26,7 +26,7 @@
 def attend(q_ref, len_ref, k_hbm, v_hbm, o_ref,
            kbuf, vbuf, q_all, q_wide, pos_rel, s_buf, p_buf, i_buf, part_o, part_l,
            pair_so, pair_ro, chip_so, chip_ro, keep_o, keep_l,
-           k_sem, v_sem, qs_sem, qr_sem, pair_sem, chip_sem):
+           k_sem, v_sem, qs_sem, qr_sem, sent_sem, pair_sem, chip_sem):
     own, num_batch, head_dim = q_ref.shape
     span = k_hbm.shape[1]
     rows = 8 * own
@@ -79,7 +79,7 @@
         if direct:
             src, peer = q_ref.at[:, part], across
         return pltpu.make_async_remote_copy(
-            src_ref=src, dst_ref=dst, send_sem=qs_sem.at[kind, c], recv_sem=qr_sem.at[kind, c],
+            src_ref=src, dst_ref=dst, send_sem=qs_sem.at[kind], recv_sem=qr_sem.at[kind, c],
             device_id={"dup": peer}, device_id_type=MESH)
 
     def q_own(c):
@@ -196,26 +196,21 @@
         total = w_mine + w_theirs
         return (w_mine * mine + w_theirs * theirs) / total, top + jnp.log2(total)
 
-    def copy_of(src, dst, sems, c, peer):
+    def pair_copy(c):
         return pltpu.make_async_remote_copy(
-            src_ref=src.at[c], dst_ref=dst.at[c], send_sem=sems.at[0, c], recv_sem=sems.at[1, c],
-            device_id={"dup": peer}, device_id_type=MESH)
-
-    def pair_copy(c):
-        return copy_of(pair_so, pair_ro, pair_sem, c, partner)
-
-    def chip_copies(c):
-        return [pltpu.make_async_remote_copy(
-            src_ref=chip_so.at[c, n], dst_ref=chip_ro.at[c, n], send_sem=chip_sem.at[0, n, c], recv_sem=chip_sem.at[1, n, c],
-            device_id={"dup": peer}, device_id_type=MESH) for n, peer in ((2, across), (0, behind), (1, ahead))]
+            src_ref=pair_so.at[c], dst_ref=pair_ro.at[c], send_sem=sent_sem.at[0], recv_sem=pair_sem.at[c],
+            device_id={"dup": partner}, device_id_type=MESH)
 
     def chip_start(c):
-        for copy in chip_copies(c):
-            copy.start()
+        for n, peer in ((2, across), (0, behind), (1, ahead)):
+            pltpu.make_async_remote_copy(
+                src_ref=chip_so.at[c, n], dst_ref=chip_ro.at[c, n], send_sem=sent_sem.at[1], recv_sem=chip_sem.at[c],
+                device_id={"dup": peer}, device_id_type=MESH).start()
 
     def chip_arrive(c):
-        for copy in chip_copies(c):
-            copy.wait_recv()
+        pltpu.make_async_remote_copy(
+            src_ref=chip_so.at[c], dst_ref=chip_ro.at[c], send_sem=sent_sem.at[1], recv_sem=chip_sem.at[c],
+            device_id={"dup": partner}, device_id_type=MESH).wait_recv()
 
     def slab(ref, g, row):
         return ref.at[g % RING][pl.ds(row * PITCH, GROUP), :]
@@ -266,14 +261,15 @@
     q_pass_far(1)
     q_pass_near(3)
 
-    def step(t, carry):
+    def step(t, carry, full):
         c = t // ASK
 
         @pl.when(t % ASK == 0)
         def _():
-            @pl.when(c + 5 < asks)
-            def _():
-                q_own(c + 5)
+            if not full:
+                @pl.when(c + 5 < asks)
+                def _():
+                    q_own(c + 5)
 
             @pl.when(c + 3 < asks)
             def _():
@@ -287,16 +283,15 @@
 
         key_copy(t).wait()
         value_copy(t - 2).wait()
-
-        @pl.when(t >= MERGE)
-        def _():
+        if full:
             pair_copy(t - MERGE).wait_recv()
-
-        @pl.when(t >= FINAL)
-        def _():
             chip_arrive(t - FINAL)
-
-        final(t - FINAL)
+            final(t - FINAL)
+        else:
+            @pl.when(t >= MERGE)
+            def _():
+                pair_copy(t - MERGE).wait_recv()
+
         merge(t - MERGE)
         mix(t - 2)
         give(t - GIVE)
@@ -304,21 +299,24 @@
         score(t)
 
         pair_copy(t - GIVE).start()
-
-        @pl.when(t >= MERGE)
-        def _():
+        if full:
             chip_start(t - MERGE)
-
-        @pl.when(t + KEYS < steps)
-        def _():
-            key_copy(t + KEYS).start()
-
-        @pl.when(t - 2 + VALUES < steps)
-        def _():
-            value_copy(t - 2 + VALUES).start()
+        else:
+            @pl.when(t >= MERGE)
+            def _():
+                chip_start(t - MERGE)
+
+            @pl.when(t + KEYS < steps)
+            def _():
+                key_copy(t + KEYS).start()
+
+            @pl.when(t - 2 + VALUES < steps)
+            def _():
+                value_copy(t - 2 + VALUES).start()
         return carry
 
-    lax.fori_loop(2, steps, step, 0)
+    lax.fori_loop(2, FINAL, functools.partial(step, full=False), 0)
+    lax.fori_loop(FINAL, steps, functools.partial(step, full=True), 0)
 
     def late_merge(g, carry):
         pair_copy(g).wait_recv()
@@ -332,31 +330,29 @@
         return carry
 
     value_copy(steps - 2).wait()
+    pair_copy(steps - 4).wait_recv()
+    merge(steps - 4)
     mix(steps - 2)
     give(steps - 2)
     soften(steps - 1)
     pair_copy(steps - 2).start()
+    chip_start(steps - 4)
     value_copy(steps - 1).wait()
     mix(steps - 1)
     give(steps - 1)
     pair_copy(steps - 1).start()
-
-    lax.fori_loop(steps - MERGE, steps, late_merge, 0)
+    lax.fori_loop(steps - MERGE + 1, steps, late_merge, 0)
     lax.fori_loop(steps - FINAL, steps, late_final, 0)
 
-    def drain_asks(c, carry):
-        for kind in range(5):
-            q_copy(kind, c).wait_send()
-        return carry
-
-    lax.fori_loop(0, asks, drain_asks, 0)
-
-    def drain(c, carry):
-        for copy in [pair_copy(c)] + chip_copies(c):
-            copy.wait_send()
-        return carry
-
-    lax.fori_loop(0, steps, drain, 0)
+    def drain(src, sem):
+        pltpu.make_async_remote_copy(
+            src_ref=src, dst_ref=src, send_sem=sem, recv_sem=pair_sem.at[0],
+            device_id={"dup": partner}, device_id_type=MESH).wait_send()
+
+    for kind, src in enumerate((q_ref, q_ref, q_ref, q_all.at[1], q_all.at[1:4])):
+        drain(src, qs_sem.at[kind])
+    drain(pair_so.at[pl.ds(0, steps)], sent_sem.at[0])
+    drain(chip_so.at[pl.ds(0, steps)], sent_sem.at[1])
 
 
 def solution(mesh):
@@ -395,8 +391,8 @@
                 pltpu.VMEM((KEEP, own, GROUP, head_dim), f32),
                 pltpu.VMEM((KEEP, own, GROUP, head_dim), f32),
                 dma((KEYS,)), dma((VALUES,)),
-                dma((5, asks)), dma((5, asks)),
-                dma((2, steps)), dma((2, 3, steps)),
+                dma((5,)), dma((5, asks)),
+                dma((2,)), dma((steps,)), dma((steps,)),
             ],
             compiler_params=pltpu.CompilerParams(
                 collective_id=0, has_side_effects=True, vmem_limit_bytes=60 * 1024 * 1024),

time: 42.3 us -> 40.1 us (0.948)
  Pallas kernels: 40.5 us -> 38.4 us
    pallas_call x1, Pallas kernels: 40.5 us -> 38.4 us  [group_step(): pl.pallas_call(attend, out_shape=jax.ShapeDtypeStruct((own, num_batch, he...]
where the time goes in v9:
time: 40.1 us; the launch traced here: 40 us
  Pallas kernels  38.4 us (96%)
  local copies, waits for them, and re-layouts  1.62 us (4%)
    pallas_call x1, Pallas kernels, group_step(): pl.pallas_call(attend, out_shape=jax.ShapeDtypeStruct((own, num_batch, he...  38.4 us
    unnamed x1, local copies, waits for them, and re-layouts  1.62 us

profile of v9, /device:TPU:112, one launch (start us, length us, event | category | flops | bytes accessed | tf_op | source)
XLA Modules:
  0.0 40.0 jit_solution(3822354212096873013)
XLA Ops:
  0.0 38.4 %shard_map.46 = bf16[3,256,128]{2,1,0:T(8,128)(2,1)} custom-call(bf16[3,256,128]{2,1,0:T(8,128)(2,1)} %bitcast.3, s32[256]{0:T(256)} %len_ref.1, bf16[256,512,128]{2,1,0:T(8,128)(2,1)} %k_hbm.1, bf16[256,512,128]{2,1,0:T(8,128)(2,1)} %v_hbm.1), custom_call_target="tpu_custom_call" | custom-call | flops 1610612736 | bytes 67108864 | tf_op jit(solution)/shard_map/pallas_call | solution.py:371
  38.4 1.6 %copy.6 = bf16[256,3,128]{2,0,1:T(8,128)(2,1)} copy(bf16[256,3,128]{2,0,1:T(8,128)(2,1)} %bitcast.2) | data formatting | bytes 393216

commit v10 on v9

--- a/solution.py
+++ b/solution.py
@@ -33,7 +33,7 @@
     half = 4 * own
     data = own * GROUP
     steps = num_batch // GROUP
-    asks = steps // ASK
+    asks = steps // ASK + 1
     scale = (head_dim ** -0.5) * LOG2E
 
     me = lax.axis_index("dup")
@@ -68,7 +68,10 @@
         pl.semaphore_signal(barrier, inc=1, device_id={"dup": peer}, device_id_type=MESH)
 
     def q_copy(kind, c, direct=False):
-        part = pl.ds(pl.multiple_of(c * ASK * GROUP, ASK * GROUP), ASK * GROUP)
+        if isinstance(c, int) and c < 2:
+            part = pl.ds(c * GROUP, GROUP)
+        else:
+            part = pl.ds(pl.multiple_of((c - 1) * ASK * GROUP, ASK * GROUP), ASK * GROUP)
         src, dst, peer = (
             (q_ref.at[:, part], q_all.at[1, :, part], behind),
             (q_ref.at[:, part], q_all.at[2, :, part], ahead),
@@ -109,14 +112,16 @@
     pos_rel[...] = lax.broadcasted_iota(jnp.int32, (rows, span), 1) + span_start - token
 
     pl.semaphore_wait(barrier, 4)
-    q_copy(3, 0, direct=True).start()
-    q_own(0)
-    for c in range(1, 6):
+    for c in range(2):
+        q_copy(3, c, direct=True).start()
         q_own(c)
-    q_copy(0, 0).wait_recv()
-    q_pass_far(0)
-    q_pass_near(1)
+    for c in range(2, 7):
+        q_own(c)
+    for c in range(2):
+        q_copy(0, c).wait_recv()
+        q_pass_far(c)
     q_pass_near(2)
+    q_pass_near(3)
 
     def q_arrive(c):
         for kind in (2, 4):
@@ -125,49 +130,51 @@
     lane = lax.broadcasted_iota(jnp.int32, (GROUP, head_dim), 1)
     seq = lax.broadcasted_iota(jnp.int32, (GROUP, head_dim), 0)
 
-    def score(g):
+    def widen(g):
         part = pl.ds(pl.multiple_of(g * GROUP, GROUP), GROUP)
         for s in range(8):
             for i in range(own):
                 block = q_ref[i, part, :] if s == 0 else q_all[s, i, part, :]
                 q_wide[pl.ds((s * own + i) * PITCH, GROUP), :] = block.astype(jnp.float32)
-        slot = g % KEYS
+
+    def score(g, n):
+        slot, j = g % KEYS, 2 * n
         zeros = jnp.zeros((rows, head_dim), jnp.float32)
-        for j in range(0, GROUP, 2):
-            q0 = q_wide[pl.ds(j, rows, stride=PITCH), :]
-            q1 = q_wide[pl.ds(j + 1, rows, stride=PITCH), :]
-            q2 = jnp.concatenate([jnp.concatenate([q0, zeros], 1), jnp.concatenate([zeros, q1], 1)], 0).astype(jnp.bfloat16)
-            k2 = jnp.concatenate([kbuf[slot, j], kbuf[slot, j + 1]], 1)
-            s_buf[j // 2] = lax.dot_general(q2, k2, (((1,), (1,)), ((), ())), preferred_element_type=jnp.float32)
-
-    def soften(g):
+        q0 = q_wide[pl.ds(j, rows, stride=PITCH), :]
+        q1 = q_wide[pl.ds(j + 1, rows, stride=PITCH), :]
+        q2 = jnp.concatenate([jnp.concatenate([q0, zeros], 1), jnp.concatenate([zeros, q1], 1)], 0).astype(jnp.bfloat16)
+        k2 = jnp.concatenate([kbuf[slot, j], kbuf[slot, j + 1]], 1)
+        s_buf[n] = lax.dot_general(q2, k2, (((1,), (1,)), ((), ())), preferred_element_type=jnp.float32)
+
+    def soften(g, n):
         slab_l = part_l.at[g % RING]
-        for j in range(0, GROUP, 2):
-            s = s_buf[j // 2]
-            rel = pos_rel[...]
-            base = g * GROUP + j
-            s = jnp.concatenate([
-                jnp.where(rel <= len_ref[base] - DRAFT, s[:rows], NEG_BIG),
-                jnp.where(rel <= len_ref[base + 1] - DRAFT, s[rows:], NEG_BIG)], 0)
-            peak = jnp.max(s, axis=1, keepdims=True)
-            p = jnp.exp2((s - peak) * scale)
-            mass = jnp.sum(p, axis=1, keepdims=True)
-            p_buf[j // 2] = p.astype(jnp.bfloat16)
-            i_buf[j // 2] = jnp.broadcast_to(1.0 / mass, (2 * rows, head_dim))
-            log_mass = jnp.broadcast_to(peak * scale + jnp.log2(mass), (2 * rows, head_dim))
-            for n in range(2):
-                slab_l[pl.ds(j + n, rows, stride=PITCH), :] = log_mass[n * rows:(n + 1) * rows]
-
-    def mix(g):
-        slot = g % VALUES
+        j = 2 * n
+        s = s_buf[n]
+        rel = pos_rel[...]
+        base = g * GROUP + j
+        s = jnp.concatenate([
+            jnp.where(rel <= len_ref[base] - DRAFT, s[:rows], NEG_BIG),
+            jnp.where(rel <= len_ref[base + 1] - DRAFT, s[rows:], NEG_BIG)], 0)
+        peak = jnp.max(s, axis=1, keepdims=True)
+        p = jnp.exp2((s - peak) * scale)
+        mass = jnp.sum(p, axis=1, keepdims=True)
+        p_buf[n] = p.astype(jnp.bfloat16)
+        i_buf[n] = jnp.broadcast_to(1.0 / mass, (2 * rows, head_dim))
+        log_mass = jnp.broadcast_to(peak * scale + jnp.log2(mass), (2 * rows, head_dim))
+        for m in range(2):
+            slab_l[pl.ds(j + m, rows, stride=PITCH), :] = log_mass[m * rows:(m + 1) * rows]
+
+    def mix(g, n):
+        slot, j = g % VALUES, 2 * n
         slab_o = part_o.at[g % RING]
-        for j in range(0, GROUP, 2):
-            v2 = jnp.concatenate([vbuf[slot, j], vbuf[slot, j + 1]], 1)
-            o2 = jnp.dot(p_buf[j // 2], v2, preferred_element_type=jnp.float32)
-            inv = i_buf[j // 2]
-            for n in range(2):
-                o = o2[n * rows:(n + 1) * rows, n * head_dim:(n + 1) * head_dim] * inv[n * rows:(n + 1) * rows]
-                slab_o[pl.ds(j + n, rows, stride=PITCH), :] = o
+        v2 = jnp.concatenate([vbuf[slot, j], vbuf[slot, j + 1]], 1)
+        o2 = jnp.dot(p_buf[n], v2, preferred_element_type=jnp.float32)
+        inv = i_buf[n]
+        for m in range(2):
+            o = o2[m * rows:(m + 1) * rows, m * head_dim:(m + 1) * head_dim] * inv[m * rows:(m + 1) * rows]
+            slab_o[pl.ds(j + m, rows, stride=PITCH), :] = o
+
+    pairs = range(GROUP // 2)
 
     def to_lanes(values):
         total = jnp.zeros((GROUP, head_dim), jnp.float32)
@@ -252,17 +259,22 @@
 
     q_arrive(0)
     key_copy(0).wait()
-    score(0)
+    widen(0)
+    for n in pairs:
+        score(0, n)
     key_copy(KEYS).start()
     key_copy(1).wait()
-    soften(0)
-    score(1)
+    q_arrive(1)
+    widen(1)
+    for n in pairs:
+        soften(0, n)
+        score(1, n)
     key_copy(KEYS + 1).start()
-    q_pass_far(1)
-    q_pass_near(3)
+    q_pass_far(2)
+    q_pass_near(4)
 
     def step(t, carry, full):
-        c = t // ASK
+        c = t // ASK + 1
 
         @pl.when(t % ASK == 0)
         def _():
@@ -292,11 +304,13 @@
             def _():
                 pair_copy(t - MERGE).wait_recv()
 
+        widen(t)
+        for n in pairs:
+            mix(t - 2, n)
+            soften(t - 1, n)
+            score(t, n)
+        give(t - GIVE)
         merge(t - MERGE)
-        mix(t - 2)
-        give(t - GIVE)
-        soften(t - 1)
-        score(t)
 
         pair_copy(t - GIVE).start()
         if full:
@@ -332,13 +346,15 @@
     value_copy(steps - 2).wait()
     pair_copy(steps - 4).wait_recv()
     merge(steps - 4)
-    mix(steps - 2)
+    for n in pairs:
+        mix(steps - 2, n)
+        soften(steps - 1, n)
     give(steps - 2)
-    soften(steps - 1)
     pair_copy(steps - 2).start()
     chip_start(steps - 4)
     value_copy(steps - 1).wait()
-    mix(steps - 1)
+    for n in pairs:
+        mix(steps - 1, n)
     give(steps - 1)
     pair_copy(steps - 1).start()
     lax.fori_loop(steps - MERGE + 1, steps, late_merge, 0)
@@ -360,7 +376,7 @@
         num_batch, own, head_dim = q_local.shape
         span = k_span.shape[1]
         steps = num_batch // GROUP
-        asks = steps // ASK
+        asks = steps // ASK + 1
         places = steps + SPARE
         block = own * GROUP + 8
         rows = 8 * own

time: 40.1 us -> 39.9 us (level)
  no operation moved by 1% of the time
where the time goes in v10:
time: 39.9 us; the launch traced here: 39.8 us
  Pallas kernels  38.2 us (96%)
  local copies, waits for them, and re-layouts  1.62 us (4%)
    pallas_call x1, Pallas kernels, group_step(): pl.pallas_call(attend, out_shape=jax.ShapeDtypeStruct((own, num_batch, he...  38.2 us
    unnamed x1, local copies, waits for them, and re-layouts  1.62 us

profile of v10, /device:TPU:112, one launch (start us, length us, event | category | flops | bytes accessed | tf_op | source)
XLA Modules:
  0.0 39.8 jit_solution(8554753300614587277)
XLA Ops:
  0.0 38.2 %shard_map.46 = bf16[3,256,128]{2,1,0:T(8,128)(2,1)} custom-call(bf16[3,256,128]{2,1,0:T(8,128)(2,1)} %bitcast.3, s32[256]{0:T(256)} %len_ref.1, bf16[256,512,128]{2,1,0:T(8,128)(2,1)} %k_hbm.1, bf16[256,512,128]{2,1,0:T(8,128)(2,1)} %v_hbm.1), custom_call_target="tpu_custom_call" | custom-call | flops 1610612736 | bytes 67108864 | tf_op jit(solution)/shard_map/pallas_call | solution.py:387
  38.2 1.6 %copy.6 = bf16[256,3,128]{2,0,1:T(8,128)(2,1)} copy(bf16[256,3,128]{2,0,1:T(8,128)(2,1)} %bitcast.2) | data formatting | bytes 393216

commit v11 on v10

--- a/solution.py
+++ b/solution.py
@@ -115,13 +115,15 @@
     for c in range(2):
         q_copy(3, c, direct=True).start()
         q_own(c)
-    for c in range(2, 7):
-        q_own(c)
+    q_own(2)
+    q_pass_near(2)
+    q_own(3)
     for c in range(2):
         q_copy(0, c).wait_recv()
         q_pass_far(c)
-    q_pass_near(2)
+    q_own(4)
     q_pass_near(3)
+    q_own(5)
 
     def q_arrive(c):
         for kind in (2, 4):
@@ -263,6 +265,7 @@
     for n in pairs:
         score(0, n)
     key_copy(KEYS).start()
+    q_pass_far(2)
     key_copy(1).wait()
     q_arrive(1)
     widen(1)
@@ -270,7 +273,7 @@
         soften(0, n)
         score(1, n)
     key_copy(KEYS + 1).start()
-    q_pass_far(2)
+    q_own(6)
     q_pass_near(4)
 
     def step(t, carry, full):

time: 39.9 us -> 41.9 us (1.050)
  Pallas kernels: 38.2 us -> 40 us
    pallas_call x1, Pallas kernels: 38.2 us -> 40 us  [group_step(): pl.pallas_call(attend, out_shape=jax.ShapeDtypeStruct((own, num_batch, he...]
where the time goes in v11:
time: 41.9 us; the launch traced here: 41.7 us
  Pallas kernels  40 us (95%)
  local copies, waits for them, and re-layouts  1.62 us (4%)
    pallas_call x1, Pallas kernels, group_step(): pl.pallas_call(attend, out_shape=jax.ShapeDtypeStruct((own, num_batch, he...  40 us
    unnamed x1, local copies, waits for them, and re-layouts  1.62 us

profile of v11, /device:TPU:112, one launch (start us, length us, event | category | flops | bytes accessed | tf_op | source)
XLA Modules:
  0.0 41.7 jit_solution(8616016558714009652)
XLA Ops:
  0.0 40.0 %shard_map.46 = bf16[3,256,128]{2,1,0:T(8,128)(2,1)} custom-call(bf16[3,256,128]{2,1,0:T(8,128)(2,1)} %bitcast.3, s32[256]{0:T(256)} %len_ref.1, bf16[256,512,128]{2,1,0:T(8,128)(2,1)} %k_hbm.1, bf16[256,512,128]{2,1,0:T(8,128)(2,1)} %v_hbm.1), custom_call_target="tpu_custom_call" | custom-call | flops 1610612736 | bytes 67108864 | tf_op jit(solution)/shard_map/pallas_call | solution.py:390
  40.0 1.6 %copy.6 = bf16[256,3,128]{2,0,1:T(8,128)(2,1)} copy(bf16[256,3,128]{2,0,1:T(8,128)(2,1)} %bitcast.2) | data formatting | bytes 393216

commit v12 on v10

--- a/solution.py
+++ b/solution.py
@@ -86,12 +86,13 @@
             device_id={"dup": peer}, device_id_type=MESH)
 
     def q_own(c):
-        for kind in (0, 1, 2):
-            q_copy(kind, c).start()
+        q_copy(0, c).start()
+        q_copy(2, c).start()
 
     def q_pass_near(c):
         q_copy(0, c).wait_recv()
         q_copy(3, c).start()
+        q_copy(1, c).start()
 
     def q_pass_far(c):
         q_copy(1, c).wait_recv()
@@ -115,12 +116,13 @@
     for c in range(2):
         q_copy(3, c, direct=True).start()
         q_own(c)
+        q_copy(1, c).start()
     for c in range(2, 7):
         q_own(c)
+    q_pass_near(2)
     for c in range(2):
         q_copy(0, c).wait_recv()
         q_pass_far(c)
-    q_pass_near(2)
     q_pass_near(3)
 
     def q_arrive(c):
@@ -263,6 +265,7 @@
     for n in pairs:
         score(0, n)
     key_copy(KEYS).start()
+    q_pass_far(2)
     key_copy(1).wait()
     q_arrive(1)
     widen(1)
@@ -270,7 +273,6 @@
         soften(0, n)
         score(1, n)
     key_copy(KEYS + 1).start()
-    q_pass_far(2)
     q_pass_near(4)
 
     def step(t, carry, full):

time: 39.9 us -> 39.9 us (level)
  no operation moved by 1% of the time
where the time goes in v12:
time: 39.9 us; the launch traced here: 39.6 us
  Pallas kernels  38 us (95%)
  local copies, waits for them, and re-layouts  1.62 us (4%)
    pallas_call x1, Pallas kernels, group_step(): pl.pallas_call(attend, out_shape=jax.ShapeDtypeStruct((own, num_batch, he...  38 us
    unnamed x1, local copies, waits for them, and re-layouts  1.62 us

profile of v12, /device:TPU:112, one launch (start us, length us, event | category | flops | bytes accessed | tf_op | source)
XLA Modules:
  0.0 39.6 jit_solution(1757610660468398612)
XLA Ops:
  0.0 38.0 %shard_map.46 = bf16[3,256,128]{2,1,0:T(8,128)(2,1)} custom-call(bf16[3,256,128]{2,1,0:T(8,128)(2,1)} %bitcast.3, s32[256]{0:T(256)} %len_ref.1, bf16[256,512,128]{2,1,0:T(8,128)(2,1)} %k_hbm.1, bf16[256,512,128]{2,1,0:T(8,128)(2,1)} %v_hbm.1), custom_call_target="tpu_custom_call" | custom-call | flops 1610612736 | bytes 67108864 | tf_op jit(solution)/shard_map/pallas_call | solution.py:389
  38.0 1.6 %copy.6 = bf16[256,3,128]{2,0,1:T(8,128)(2,1)} copy(bf16[256,3,128]{2,0,1:T(8,128)(2,1)} %bitcast.2) | data formatting | bytes 393216

commit v13 on v12

--- a/solution.py
+++ b/solution.py
@@ -19,8 +19,8 @@
 RING = 8
 KEEP = 16
 ASK = 2
-GIVE, MERGE, FINAL = 2, 4, 9
-SPARE = 9
+GIVE, MERGE = 2, 4
+SPARE = 4
 
 
 def attend(q_ref, len_ref, k_hbm, v_hbm, o_ref,
@@ -299,8 +299,6 @@
         value_copy(t - 2).wait()
         if full:
             pair_copy(t - MERGE).wait_recv()
-            chip_arrive(t - FINAL)
-            final(t - FINAL)
         else:
             @pl.when(t >= MERGE)
             def _():
@@ -331,8 +329,8 @@
                 value_copy(t - 2 + VALUES).start()
         return carry
 
-    lax.fori_loop(2, FINAL, functools.partial(step, full=False), 0)
-    lax.fori_loop(FINAL, steps, functools.partial(step, full=True), 0)
+    lax.fori_loop(2, steps // 2, functools.partial(step, full=False), 0)
+    lax.fori_loop(steps // 2, steps, functools.partial(step, full=True), 0)
 
     def late_merge(g, carry):
         pair_copy(g).wait_recv()
@@ -360,7 +358,7 @@
     give(steps - 1)
     pair_copy(steps - 1).start()
     lax.fori_loop(steps - MERGE + 1, steps, late_merge, 0)
-    lax.fori_loop(steps - FINAL, steps, late_final, 0)
+    lax.fori_loop(0, steps, late_final, 0)
 
     def drain(src, sem):
         pltpu.make_async_remote_copy(

time: 39.9 us -> 39.6 us (level)
  no operation moved by 1% of the time
where the time goes in v13:
time: 39.6 us; the launch traced here: 39.3 us
  Pallas kernels  37.7 us (95%)
  local copies, waits for them, and re-layouts  1.62 us (4%)
    pallas_call x1, Pallas kernels, group_step(): pl.pallas_call(attend, out_shape=jax.ShapeDtypeStruct((own, num_batch, he...  37.7 us
    unnamed x1, local copies, waits for them, and re-layouts  1.62 us

profile of v13, /device:TPU:112, one launch (start us, length us, event | category | flops | bytes accessed | tf_op | source)
XLA Modules:
  0.0 39.3 jit_solution(12991212598610803227)
XLA Ops:
  0.0 37.7 %shard_map.46 = bf16[3,256,128]{2,1,0:T(8,128)(2,1)} custom-call(bf16[3,256,128]{2,1,0:T(8,128)(2,1)} %bitcast.3, s32[256]{0:T(256)} %len_ref.1, bf16[256,512,128]{2,1,0:T(8,128)(2,1)} %k_hbm.1, bf16[256,512,128]{2,1,0:T(8,128)(2,1)} %v_hbm.1), custom_call_target="tpu_custom_call" | custom-call | flops 1610612736 | bytes 67108864 | tf_op jit(solution)/shard_map/pallas_call | solution.py:387
  37.7 1.6 %copy.6 = bf16[256,3,128]{2,0,1:T(8,128)(2,1)} copy(bf16[256,3,128]{2,0,1:T(8,128)(2,1)} %bitcast.2) | data formatting | bytes 393216

commit v14 on v13

--- a/solution.py
+++ b/solution.py
@@ -19,8 +19,8 @@
 RING = 8
 KEEP = 16
 ASK = 2
-GIVE, MERGE = 2, 4
-SPARE = 4
+GIVE, MERGE = 2, 5
+SPARE = 5
 
 
 def attend(q_ref, len_ref, k_hbm, v_hbm, o_ref,
@@ -344,20 +344,23 @@
         return carry
 
     value_copy(steps - 2).wait()
-    pair_copy(steps - 4).wait_recv()
-    merge(steps - 4)
+    pair_copy(steps - MERGE).wait_recv()
+    merge(steps - MERGE)
     for n in pairs:
         mix(steps - 2, n)
         soften(steps - 1, n)
     give(steps - 2)
     pair_copy(steps - 2).start()
-    chip_start(steps - 4)
+    chip_start(steps - MERGE)
     value_copy(steps - 1).wait()
+    pair_copy(steps - MERGE + 1).wait_recv()
+    merge(steps - MERGE + 1)
     for n in pairs:
         mix(steps - 1, n)
     give(steps - 1)
     pair_copy(steps - 1).start()
-    lax.fori_loop(steps - MERGE + 1, steps, late_merge, 0)
+    chip_start(steps - MERGE + 1)
+    lax.fori_loop(steps - MERGE + 2, steps, late_merge, 0)
     lax.fori_loop(0, steps, late_final, 0)
 
     def drain(src, sem):

time: 39.6 us -> 39.8 us (level)
  no operation moved by 1% of the time
where the time goes in v14:
time: 39.8 us; the launch traced here: 39.7 us
  Pallas kernels  38 us (95%)
  local copies, waits for them, and re-layouts  1.62 us (4%)
    pallas_call x1, Pallas kernels, group_step(): pl.pallas_call(attend, out_shape=jax.ShapeDtypeStruct((own, num_batch, he...  38 us
    unnamed x1, local copies, waits for them, and re-layouts  1.62 us

profile of v14, /device:TPU:112, one launch (start us, length us, event | category | flops | bytes accessed | tf_op | source)
XLA Modules:
  0.0 39.7 jit_solution(17189314983391974146)
XLA Ops:
  0.0 38.0 %shard_map.46 = bf16[3,256,128]{2,1,0:T(8,128)(2,1)} custom-call(bf16[3,256,128]{2,1,0:T(8,128)(2,1)} %bitcast.3, s32[256]{0:T(256)} %len_ref.1, bf16[256,512,128]{2,1,0:T(8,128)(2,1)} %k_hbm.1, bf16[256,512,128]{2,1,0:T(8,128)(2,1)} %v_hbm.1), custom_call_target="tpu_custom_call" | custom-call | flops 1610612736 | bytes 67108864 | tf_op jit(solution)/shard_map/pallas_call | solution.py:390
  38.1 1.6 %copy.6 = bf16[256,3,128]{2,0,1:T(8,128)(2,1)} copy(bf16[256,3,128]{2,0,1:T(8,128)(2,1)} %bitcast.2) | data formatting | bytes 393216

commit v15 on v13

--- a/solution.py
+++ b/solution.py
@@ -120,10 +120,12 @@
     for c in range(2, 7):
         q_own(c)
     q_pass_near(2)
-    for c in range(2):
-        q_copy(0, c).wait_recv()
-        q_pass_far(c)
+    q_copy(0, 0).wait_recv()
+    q_pass_far(0)
     q_pass_near(3)
+    q_copy(0, 1).wait_recv()
+    q_pass_far(1)
+    q_pass_near(4)
 
     def q_arrive(c):
         for kind in (2, 4):
@@ -273,8 +275,6 @@
         soften(0, n)
         score(1, n)
     key_copy(KEYS + 1).start()
-    q_pass_near(4)
-
     def step(t, carry, full):
         c = t // ASK + 1
 

time: 39.6 us -> 39.3 us (level)
  no operation moved by 1% of the time
where the time goes in v15:
time: 39.3 us; the launch traced here: 39.1 us
  Pallas kernels  37.5 us (95%)
  local copies, waits for them, and re-layouts  1.62 us (4%)
    pallas_call x1, Pallas kernels, group_step(): pl.pallas_call(attend, out_shape=jax.ShapeDtypeStruct((own, num_batch, he...  37.5 us
    unnamed x1, local copies, waits for them, and re-layouts  1.62 us

profile of v15, /device:TPU:112, one launch (start us, length us, event | category | flops | bytes accessed | tf_op | source)
XLA Modules:
  0.0 39.1 jit_solution(5228761957429227299)
XLA Ops:
  0.0 37.5 %shard_map.46 = bf16[3,256,128]{2,1,0:T(8,128)(2,1)} custom-call(bf16[3,256,128]{2,1,0:T(8,128)(2,1)} %bitcast.3, s32[256]{0:T(256)} %len_ref.1, bf16[256,512,128]{2,1,0:T(8,128)(2,1)} %k_hbm.1, bf16[256,512,128]{2,1,0:T(8,128)(2,1)} %v_hbm.1), custom_call_target="tpu_custom_call" | custom-call | flops 1610612736 | bytes 67108864 | tf_op jit(solution)/shard_map/pallas_call | solution.py:387
  37.5 1.6 %copy.6 = bf16[256,3,128]{2,0,1:T(8,128)(2,1)} copy(bf16[256,3,128]{2,0,1:T(8,128)(2,1)} %bitcast.2) | data formatting | bytes 393216
